TPU v7x, 32 devices: a whole 2x2x4 slice. The times are simulated.
32 devices in a mesh: mission: 2 (over x), arc: 16 (over z, y, core).
Axes of the slice: x: 2, y: 2, z: 4, core: 2. Of those that a mesh axis runs over, the one named last changes fastest.
Arguments:
- design: bfloat16 [2560, 5120], P(('mission', 'arc')), may hold values from -3 to 3
- nuisance_design: bfloat16 [2560, 128], P(('mission', 'arc')), may hold values from -1 to 1
- observed: float32 [2560], P(('mission', 'arc')), may hold values from -6 to 6
- arc_of_row: int32 [2560], P(('mission', 'arc')), may hold values from 0 to 1, as said below
- nuis_size: int32 [64], P(('mission', 'arc')), may hold values from 32 to 128
- weight_index: int32 [2560], P(('mission', 'arc')), may hold values from 0 to 7
- kind_weight: float32 [8], replicated, may hold values from 0.3 to 3
- mission_weight: float32 [2], P('mission'), may hold values from 0.3 to 3
Outputs:
- normal_fold: float32 [2560, 5120], P(('mission', 'arc'))
- right_side: float32 [5120], P(('mission', 'arc'))
- tail_diagonal: float32 [2560], P(('mission', 'arc'))
Inputs may be any that keep to these rules, and one draw needn't show every extreme that they name: `arc_of_row`: in each row block of 80 rows the rows of arc 0 come first and those of arc 1 follow; each arc has at least 20 rows.
All inputs are finite; a program needn't handle non-finite values.
Results may differ from a plain program's by a relative error of at most 0.019.
Values may be sent and summed in bfloat16 or wider, within the bound.
A program may use at most 192 MiB of HBM per device.

v0:
```python
import functools

import jax
import jax.numpy as jnp
import numpy as np
from jax import lax
from jax.experimental import pallas as pl
from jax.experimental.pallas import tpu as pltpu
from jax.sharding import PartitionSpec as P

LANES = 128


def rounded_up(value, unit):
    return -(-value // unit) * unit


def projector_kernel(
    sizes_ref, kinds_ref, nuis_ref, arc_col_ref, arc_row_ref, kind_col_ref, obs_row_ref, out_ref
):
    rows, wide = out_ref.shape
    arc_col = arc_col_ref[...]
    kind_col = kind_col_ref[...]
    weight = jnp.zeros((rows, 1), jnp.float32)
    for kind in range(kinds_ref.shape[0]):
        weight = jnp.where(kind_col == kind, kinds_ref[kind], weight)
    size = jnp.zeros((rows, 1), jnp.int32)
    for arc in range(sizes_ref.shape[0]):
        size = jnp.where(arc_col == arc, sizes_ref[arc], size)
    nuis = nuis_ref[...].astype(jnp.float32)
    nuis = jnp.where(lax.broadcasted_iota(jnp.int32, nuis.shape, 1) < size, nuis, 0.0)
    padded = jnp.concatenate(
        [nuis, jnp.zeros((wide - rows, nuis.shape[1]), jnp.float32)], axis=0
    )
    gram = lax.dot_general(
        nuis.astype(jnp.bfloat16),
        padded.astype(jnp.bfloat16),
        (((1,), (1,)), ((), ())),
        preferred_element_type=jnp.float32,
    )
    lane = lax.broadcasted_iota(jnp.int32, (rows, wide), 1)
    sub = lax.broadcasted_iota(jnp.int32, (rows, wide), 0)
    state = jnp.where(arc_col == arc_row_ref[...], gram, 0.0)
    state = state + jnp.where(lane == sub, 1.0 / weight, 0.0)
    for k in range(rows):
        row = state[k : k + 1, :]
        col = state[:, k : k + 1]
        inv = 1.0 / row[:, k : k + 1]
        scaled_row = row * inv
        scaled_col = col * inv
        swept = state - col * scaled_row
        swept = jnp.where(lane == k, scaled_col, swept)
        swept = jnp.where(sub == k, scaled_row, swept)
        state = jnp.where((lane == k) & (sub == k), -inv, swept)
    inverse = -state
    reduced_obs = jnp.sum(inverse * obs_row_ref[...], axis=1, keepdims=True)
    out_ref[...] = jnp.where(lane == rows, reduced_obs, inverse).astype(out_ref.dtype)


def fold_kernel(
    block_rows,
    width,
    with_right,
    weight_ref,
    span_ref,
    proj_ref,
    picked_ref,
    perm_ref,
    rows_ref,
    above_ref,
    mirror_ref,
    fold_ref,
    tail_ref,
    *rest,
):
    lhs_ref = rest[-1]
    tile = pl.program_id(0)
    tile_cols = above_ref.shape[1]
    out_rows = fold_ref.shape[0]
    weight = weight_ref[0]

    @pl.when(tile == 0)
    def _():
        tail = jnp.zeros((1, width), jnp.float32)
        lane = lax.broadcasted_iota(jnp.int32, (block_rows, width), 1)
        pieces = []
        for block in range(proj_ref.shape[0] // block_rows):
            span = pl.ds(block * block_rows, block_rows)
            proj = proj_ref[span, :]
            picked = picked_ref[span, :]
            reduced = lax.dot_general(
                proj[:, :block_rows], picked, (((1,), (0,)), ((), ())),
                preferred_element_type=jnp.float32,
            )
            tail_reduced = reduced[:, 2 * width :].astype(jnp.bfloat16).astype(jnp.float32)
            tail += jnp.sum(
                picked[:, 2 * width :].astype(jnp.float32) * tail_reduced, axis=0, keepdims=True
            )
            first = jnp.where(
                lane == width - 1,
                proj[:, block_rows : block_rows + 1].astype(jnp.float32),
                reduced[:, :width],
            )
            second = jnp.dot(
                reduced[:, width : 2 * width].astype(jnp.bfloat16),
                perm_ref[...],
                preferred_element_type=jnp.float32,
            )
            pieces.append(jnp.concatenate([first, second], axis=1))
        lhs_ref[...] = jnp.concatenate(pieces, axis=0).T.astype(jnp.bfloat16)
        tail_ref[...] = weight * tail

    low, high = span_ref[0], span_ref[1]
    col_start = tile * tile_cols
    all_above = col_start >= high
    all_mirror = col_start + tile_cols <= low

    def above_tile():
        return weight * jnp.dot(
            lhs_ref[pl.ds(0, width), :], above_ref[...], preferred_element_type=jnp.float32
        )

    def mirror_tile():
        mirror = jnp.dot(
            lhs_ref[pl.ds(width, rounded_up(out_rows, 16)), :],
            mirror_ref[...],
            preferred_element_type=jnp.float32,
        )[:out_rows]
        mirror = (weight * mirror).astype(jnp.bfloat16)
        flip = (
            lax.broadcasted_iota(jnp.int32, (LANES, LANES), 0)
            + lax.broadcasted_iota(jnp.int32, (LANES, LANES), 1)
            == LANES - 1
        ).astype(jnp.float32).astype(jnp.bfloat16)
        return jnp.concatenate(
            [
                jnp.dot(
                    mirror[:, start : start + LANES], flip, preferred_element_type=jnp.float32
                )
                for start in range(tile_cols - LANES, -1, -LANES)
            ],
            axis=1,
        )

    if with_right:
        above = above_tile()
        rest[0][...] = above[width - 1 : width, :]
        fold_ref[...] = above[:out_rows].astype(fold_ref.dtype)
    else:

        @pl.when(jnp.logical_not(all_mirror))
        def _():
            fold_ref[...] = above_tile()[:out_rows].astype(fold_ref.dtype)

    @pl.when(all_mirror)
    def _():
        fold_ref[...] = mirror_tile().astype(fold_ref.dtype)

    @pl.when(jnp.logical_not(jnp.logical_or(all_above, all_mirror)))
    def _():
        cols = lax.broadcasted_iota(jnp.int32, (out_rows, tile_cols), 1) + col_start
        fold_ref[...] = jnp.where(
            cols >= rows_ref[...], fold_ref[...].astype(jnp.float32), mirror_tile()
        ).astype(fold_ref.dtype)


def on_device(
    design,
    nuisance_design,
    observed,
    arc_of_row,
    nuis_size,
    weight_index,
    kind_weight,
    mission_weight,
):
    groups = lax.axis_size("mission")
    members = lax.axis_size("arc")
    group = lax.axis_index("mission")
    member = lax.axis_index("arc")
    block_rows, width_all = design.shape
    half_width = width_all // 2
    final_rows = half_width // (groups * members)
    wide = rounded_up(block_rows + 1, LANES)
    inner = 2 if members % 2 == 0 else 1
    outer = 4 if members % (4 * inner) == 0 else 1
    mid = members // (outer * inner)
    mid_at = (member // inner) % mid
    gather_groups = [
        [(o * mid + y) * inner + c for o in range(outer) for c in range(inner)]
        for y in range(mid)
    ]

    def gathered(array):
        return lax.all_gather(
            array, "arc", axis=0, tiled=True, axis_index_groups=gather_groups
        )

    def member_of(y):
        return (member // (inner * mid) * mid + y) * inner + member % inner

    vmem = pl.BlockSpec(memory_space=pltpu.VMEM)
    smem = pl.BlockSpec(memory_space=pltpu.SMEM)

    design_all = gathered(design)

    proj = pl.pallas_call(
        projector_kernel,
        out_shape=jax.ShapeDtypeStruct((block_rows, wide), jnp.bfloat16),
        in_specs=[smem, smem, vmem, vmem, vmem, vmem, vmem],
        out_specs=vmem,
        cost_estimate=pl.CostEstimate(flops=10_000_000, bytes_accessed=100_000, transcendentals=0),
        name="projector",
    )(
        nuis_size,
        kind_weight,
        nuisance_design,
        arc_of_row[:, None],
        jnp.pad(arc_of_row, (0, wide - block_rows), constant_values=-1)[None, :],
        weight_index[:, None],
        jnp.pad(observed, (0, wide - block_rows))[None, :],
    )
    proj_all = gathered(proj)

    shifts = [(dm, dy) for dm in range(groups) for dy in range(mid)]
    shifts.sort(key=lambda shift: (shift[0] == 0, shift[1] == 0))
    per_call = max(1, len(shifts) // 2)
    out_rows = per_call * final_rows
    width = rounded_up(out_rows + 1, LANES)
    place = np.arange(out_rows)
    perm = np.zeros((width, width), np.float32)
    perm[(place // final_rows) * final_rows + final_rows - 1 - place % final_rows, place] = 1.0
    tile_cols = 512
    tiles = width_all // tile_cols
    all_rows = design_all.shape[0]
    right_cols = width_all // (groups * members)
    whole = lambda shape: pl.BlockSpec(shape, lambda j: (0, 0))

    def fold_call(owners, with_right):
        def picked(start_of):
            parts = [
                lax.dynamic_slice_in_dim(design_all, start_of(owner), final_rows, 1)
                for owner in owners
            ]
            blank = jnp.zeros((all_rows, width - out_rows), design_all.dtype)
            return parts + [blank]

        picked_all = jnp.concatenate(
            picked(lambda block: block * final_rows)
            + picked(lambda block: width_all - (block + 1) * final_rows)
            + picked(lambda block: half_width + block * final_rows),
            axis=1,
        )
        starts = jnp.stack(owners).astype(jnp.int32) * final_rows
        row_ids = (
            starts[:, None] + jnp.arange(final_rows, dtype=jnp.int32)[None, :]
        ).reshape(out_rows, 1)
        span = jnp.stack([jnp.min(starts), jnp.max(starts) + final_rows - 1])
        out_shape = [
            jax.ShapeDtypeStruct((out_rows, width_all), jnp.bfloat16),
            jax.ShapeDtypeStruct((1, width), jnp.float32),
        ]
        out_specs = [
            pl.BlockSpec((out_rows, tile_cols), lambda j: (0, j)),
            whole((1, width)),
        ]
        if with_right:
            out_shape.append(jax.ShapeDtypeStruct((1, width_all), jnp.float32))
            out_specs.append(pl.BlockSpec((1, tile_cols), lambda j: (0, j)))
        return pl.pallas_call(
            functools.partial(fold_kernel, block_rows, width, with_right),
            grid=(tiles,),
            out_shape=tuple(out_shape),
            in_specs=[
                smem,
                smem,
                whole((all_rows, wide)),
                whole((all_rows, 3 * width)),
                whole((width, width)),
                whole((out_rows, 1)),
                pl.BlockSpec((all_rows, tile_cols), lambda j: (0, j)),
                pl.BlockSpec((all_rows, tile_cols), lambda j: (0, tiles - 1 - j)),
            ],
            out_specs=tuple(out_specs),
            scratch_shapes=[pltpu.VMEM((2 * width, all_rows), jnp.bfloat16)],
            compiler_params=pltpu.CompilerParams(
                dimension_semantics=("arbitrary",), vmem_limit_bytes=60 * 2**20
            ),
            cost_estimate=pl.CostEstimate(
                flops=4 * width * all_rows * width_all,
                bytes_accessed=4 * all_rows * width_all,
                transcendentals=0,
            ),
            name="fold",
        )(
            mission_weight,
            span,
            proj_all,
            picked_all,
            jnp.asarray(perm, jnp.bfloat16),
            row_ids,
            design_all,
            design_all,
        )

    def ring(dm, dy):
        pairs = []
        for m in range(groups):
            for a in range(members):
                o, y, c = a // (inner * mid), (a // inner) % mid, a % inner
                target = (o * mid + (y + dy) % mid) * inner + c
                pairs.append((m * members + a, (m + dm) % groups * members + target))
        return pairs

    right = None
    folds, vectors = [], []
    for first in range(0, len(shifts), per_call):
        here = shifts[first : first + per_call]
        owners = [
            (group + dm) % groups * members + member_of((mid_at + dy) % mid) for dm, dy in here
        ]
        fold, tail, *extra = fold_call(owners, right is None)
        if right is None:
            right = extra[0][0]
        for at, (dm, dy) in enumerate(here):
            rows = slice(at * final_rows, (at + 1) * final_rows)
            block = fold[rows]
            vector = jnp.concatenate(
                [
                    lax.dynamic_slice_in_dim(right, owners[at] * right_cols, right_cols),
                    tail[0, rows],
                ]
            )
            if dm or dy:
                block = lax.ppermute(block, ("mission", "arc"), ring(dm, dy))
                vector = lax.ppermute(vector, ("mission", "arc"), ring(dm, dy))
            folds.append(block.astype(jnp.float32))
            vectors.append(vector)
    fold_total = functools.reduce(jnp.add, folds)
    vector_total = functools.reduce(jnp.add, vectors)
    return (fold_total, vector_total[:right_cols], vector_total[right_cols:])


def solution(mesh):
    placed = (
        P(("mission", "arc"), None),
        P(("mission", "arc"), None),
        P(("mission", "arc")),
        P(("mission", "arc")),
        P(("mission", "arc")),
        P(("mission", "arc")),
        P(),
        P("mission"),
    )
    return jax.shard_map(
        on_device,
        mesh=mesh,
        in_specs=placed,
        out_specs=(P(("mission", "arc"), None), P(("mission", "arc")), P(("mission", "arc"))),
        check_vma=False,
    )
```

profile of v0, /device:TPU:0, one launch (start us, length us, event | category | flops | bytes accessed | tf_op | source)
XLA Modules:
  0.0 154.6 jit_solution(13097765995718346042)
XLA Ops:
  7.2 0.7 all-gather.2.cloned.1.call-update
  8.1 0.8 fusion
  8.9 0.8 add.278.rows_ref
  9.7 1.4 copy.15.arc_col_ref
  11.1 1.4 copy.16.kind_col_ref
  13.2 0.8 add.279.rows_ref
  15.3 1.2 pad_bitcast_fusion.1.arc_row_ref
  16.5 1.2 pad_bitcast_fusion.obs_row_ref
  17.7 12.3 %projector.1 = bf16[80,128]{1,0:T(8,128)(2,1)} custom-call(s32[2]{0:T(128)} %sizes_ref.1, f32[8]{0:T(128)} %kinds_ref.1, bf16[80,128]{1,0:T(8,128)(2,1)} %nuis_ref.1, s32[80,1]{1,0:T(8,128)} %copy.15.arc_col_ref, s32[1,128]{1,0:T(1,128)} %pad_bitcast_fusion.1.arc_row_ref, s32[80,1]{1,0:T(8,128)} %copy.16.kind_col_ref, f32[1,128]{1,0:T(1,128)} %pad_bitcast_fusion.obs_row_ref), custom_call_target="tpu_custom_call" | custom-call | flops 10000000 | bytes 100000 | tf_op jit(solution)/shard_map/projector/pallas_call | solution.py:207
  30.0 18.3 %all_gather.6.proj_ref = bf16[640,128]{1,0:T(8,128)(2,1)} all-gather(bf16[80,128]{1,0:T(8,128)(2,1)} %projector.1), channel_id=1, replica_groups={{0,1,4,5,8,9,12,13},{2,3,6,7,10,11,14,15},{16,17,20,21,24,25,28,29},{18..., dimensions={0}, use_global_device_ids=true | all-gather | bytes 184320 | tf_op jit(solution)/shard_map/all_gather | solution.py:195
  48.2 1.3 pad_add_fusion.span_ref
  49.5 1.2 pad_add_fusion.1.span_ref
  50.7 29.8 %all-gather.2.cloned.1.call-done.above_ref.mirror_ref = bf16[640,5120]{1,0:T(8,128)(2,1)} async-done(((bf16[80,5120]{1,0:T(8,128)(2,1)}), bf16[640,5120]{1,0:T(8,128)(2,1)}) %all-gather.2.cloned.1.call-update) | async-done | bytes 6553616 | tf_op jit(solution)/shard_map/all_gather | solution.py:195
  80.5 3.8 %constant_dynamic-slice_fusion.10 = (bf16[640,80]{1,0:T(8,128)(2,1)S(1)}, bf16[640,80]{1,0:T(8,128)(2,1)}, bf16[640,80]{1,0:T(8,128)(2,1)}, bf16[640,80]{1,0:T(8...) fusion(bf16[640,5120]{1,0:T(8,128)(2,1)} %all-gather.2.cloned.1, ...), kind=kLoop, calls=%fused_computation.11 | loop fusion | bytes 2457648 | tf_op jit(solution)/shard_map/dynamic_slice | solution.py:242
  84.3 3.3 %concatenate.26.picked_ref = bf16[640,768]{1,0:T(8,128)(2,1)} concatenate(bf16[640,80]{1,0:T(8,128)(2,1)S(1)} %get-tuple-element.30, bf16[640,80]{1,0:T(8,128)(2,1)S(1)} %get-tuple-element.29, bf16[640,96]{1,0:T(8,128)(2,1)S(1)} %broadcast.35, bf16[640,80]{1,0:T(8,128)(2,1)S(1)} %get-tuple-element.28, bf16[640,80]{1,0:T(8,128)(2,1)S(1)} %get-tuple-element.27, ...), dimensions={1} | concatenate | bytes 1966080 | tf_op jit(solution)/shard_map/concatenate | solution.py:248
  87.7 12.6 %fold.2 = (bf16[160,5120]{1,0:T(8,128)(2,1)}, f32[1,256]{1,0:T(1,128)}, f32[1,5120]{1,0:T(1,128)}) custom-call(f32[1]{0:T(128)S(6)} %copy.19.weight_ref, s32[2]{0:T(128)} %pad_add_fusion.span_ref, bf16[640,128]{1,0:T(8,128)(2,1)} %all_gather.6.proj_ref, bf16[640,768]{1,0:T(8,128)(2,1)} %concatenate.26.picked_ref, bf16[256,256]{1,0:T(8,128)(2,1)} %constant.126.clone.perm_ref, ...), custom_call_target="tpu_custom_call" | custom-call | flops 3355443200 | bytes 13107200 | tf_op jit(solution)/shard_map/fold/pallas_call | solution.py:270
  100.2 0.8 slice_bitcast_fusion.2
  101.0 1.5 fusion.2
  102.5 2.1 %collective-permute-start = (bf16[80,5120]{1,0:T(8,128)(2,1)S(1)}, bf16[80,5120]{1,0:T(8,128)(2,1)S(1)}, u32[]{:S(2)}, u32[]{:S(2)}) collective-permute-start(bf16[80,5120]{1,0:T(8,128)(2,1)S(1)} %get-tuple-element.31), channel_id=1, source_target_pairs={{0,18},{1,19},{2,16},{3,17},{4,22},{5,23},{6,20},{7,21},{8,26},{9,... | collective-permute-start | bytes 2457608 | tf_op jit(solution)/shard_map/ppermute | solution.py:335
  104.7 0.9 collective-permute-start.1
  105.6 3.3 %concatenate.27.picked_ref = bf16[640,768]{1,0:T(8,128)(2,1)} concatenate(bf16[640,80]{1,0:T(8,128)(2,1)} %get-tuple-element.25, bf16[640,80]{1,0:T(8,128)(2,1)} %get-tuple-element.24, bf16[640,96]{1,0:T(8,128)(2,1)S(1)} %broadcast.35, bf16[640,80]{1,0:T(8,128)(2,1)} %get-tuple-element.23, bf16[640,80]{1,0:T(8,128)(2,1)} %get-tuple-element.22, bf16[640,96]{1,0:T(8,128)(2,1)S(1)} %broadcast.35, ...), dimensions={1} | concatenate | bytes 1966080 | tf_op jit(solution)/shard_map/concatenate | solution.py:248
  108.8 12.3 %fold.3 = (bf16[160,5120]{1,0:T(8,128)(2,1)}, f32[1,256]{1,0:T(1,128)}) custom-call(f32[1]{0:T(128)S(6)} %copy.19.weight_ref, s32[2]{0:T(128)} %pad_add_fusion.1.span_ref, bf16[640,128]{1,0:T(8,128)(2,1)} %all_gather.6.proj_ref, bf16[640,768]{1,0:T(8,128)(2,1)} %concatenate.27.picked_ref, bf16[256,256]{1,0:T(8,128)(2,1)} %constant.126.clone.perm_ref, ...), custom_call_target="tpu_custom_call" | custom-call | flops 3355443200 | bytes 13107200 | tf_op jit(solution)/shard_map/fold/pallas_call | solution.py:270
  121.1 1.3 slice.32
  122.4 0.6 collective-permute-start.2
  123.0 0.8 constant_dynamic-slice_fusion.2
  123.9 1.1 collective-permute-start.4
  125.1 1.8 %collective-permute-start.3 = (f32[240]{0:T(256)S(1)}, f32[240]{0:T(256)S(1)}, u32[]{:S(2)}, u32[]{:S(2)}) collective-permute-start(f32[240]{0:T(256)S(1)} %pad_maximum_fusion), channel_id=1, source_target_pairs={{0,18},{1,19},{2,16},{3,17},{4,22},{5,23},{6,20},{7,21},{8,26},{9,... | collective-permute-start | bytes 2888 | tf_op jit(solution)/shard_map/ppermute | solution.py:336
  127.1 14.9 %collective-permute-done.4 = f32[240]{0:T(256)S(1)} collective-permute-done((f32[240]{0:T(256)S(1)}, f32[240]{0:T(256)S(1)}, u32[]{:S(2)}, u32[]{:S(2)}) %collective-permute-start.4) | collective-permute-done | bytes 992 | tf_op jit(solution)/shard_map/ppermute | solution.py:336
  142.0 0.6 collective-permute-start.5
  142.5 3.0 %collective-permute-done.5 = f32[240]{0:T(256)S(1)} collective-permute-done((f32[240]{0:T(256)S(1)}, f32[240]{0:T(256)S(1)}, u32[]{:S(2)}, u32[]{:S(2)}) %collective-permute-start.5) | collective-permute-done | bytes 992 | tf_op jit(solution)/shard_map/ppermute | solution.py:336
  145.6 0.6 slice.39
  146.2 1.5 convert_add_fusion
  (19 shorter events, 0.6 us)
Async XLA Ops:
  7.2 73.3 %all-gather.2.cloned.1.call-start = ((), (), s32[]{:S(2)}) async-start(), calls=%async_computation | async-start | bytes 7372800 | tf_op jit(solution)/shard_map/all_gather | solution.py:195
  102.5 43.6 %collective-permute-start = (bf16[80,5120]{1,0:T(8,128)(2,1)S(1)}, bf16[80,5120]{1,0:T(8,128)(2,1)S(1)}, u32[]{:S(2)}, u32[]{:S(2)}) collective-permute-start(bf16[80,5120]{1,0:T(8,128)(2,1)S(1)} %get-tuple-element.31), channel_id=1, source_target_pairs={{0,18},{1,19},{2,16},{3,17},{4,22},{5,23},{6,20},{7,21},{8,26},{9,... | collective-permute-start | bytes 2457608 | tf_op jit(solution)/shard_map/ppermute | solution.py:335
  104.7 41.5 %collective-permute-start.1 = (bf16[80,5120]{1,0:T(8,128)(2,1)S(1)}, bf16[80,5120]{1,0:T(8,128)(2,1)S(1)}, u32[]{:S(2)}, u32[]{:S(2)}) collective-permute-start(bf16[80,5120]{1,0:T(8,128)(2,1)S(1)} %get-tuple-element.32), channel_id=1, source_target_pairs={{0,16},{1,17},{2,18},{3,19},{4,20},{5,21},{6,22},{7,23},{8,24},{9,... | collective-permute-start | bytes 2457608 | tf_op jit(solution)/shard_map/ppermute | solution.py:335
  121.1 5.9 %copy-start.1 = (f32[1,256]{1,0:T(1,128)S(1)}, f32[1,256]{1,0:T(1,128)}, u32[]{:S(2)}) copy-start(f32[1,256]{1,0:T(1,128)} %get-tuple-element.12) | copy-start | bytes 3076
  121.1 25.1 %copy-start = (bf16[160,5120]{1,0:T(8,128)(2,1)S(1)}, bf16[160,5120]{1,0:T(8,128)(2,1)}, u32[]{:S(2)}) copy-start(bf16[160,5120]{1,0:T(8,128)(2,1)} %get-tuple-element.9) | copy-start | bytes 4915204
  122.4 23.8 %collective-permute-start.2 = (bf16[80,5120]{1,0:T(8,128)(2,1)S(1)}, bf16[80,5120]{1,0:T(8,128)(2,1)S(1)}, u32[]{:S(2)}, u32[]{:S(2)}) collective-permute-start(bf16[80,5120]{1,0:T(8,128)(2,1)S(1)} %slice.32), channel_id=1, source_target_pairs={{0,2},{1,3},{2,0},{3,1},{4,6},{5,7},{6,4},{7,5},{8,10},{9,11},{10,... | collective-permute-start | bytes 2457608 | tf_op jit(solution)/shard_map/ppermute | solution.py:335
  123.9 18.0 %collective-permute-start.4 = (f32[240]{0:T(256)S(1)}, f32[240]{0:T(256)S(1)}, u32[]{:S(2)}, u32[]{:S(2)}) collective-permute-start(f32[240]{0:T(256)S(1)} %pad_maximum_fusion.1), channel_id=1, source_target_pairs={{0,16},{1,17},{2,18},{3,19},{4,20},{5,21},{6,22},{7,23},{8,24},{9,... | collective-permute-start | bytes 2888 | tf_op jit(solution)/shard_map/ppermute | solution.py:336
  125.1 17.4 %collective-permute-start.3 = (f32[240]{0:T(256)S(1)}, f32[240]{0:T(256)S(1)}, u32[]{:S(2)}, u32[]{:S(2)}) collective-permute-start(f32[240]{0:T(256)S(1)} %pad_maximum_fusion), channel_id=1, source_target_pairs={{0,18},{1,19},{2,16},{3,17},{4,22},{5,23},{6,20},{7,21},{8,26},{9,... | collective-permute-start | bytes 2888 | tf_op jit(solution)/shard_map/ppermute | solution.py:336
  142.0 3.6 %collective-permute-start.5 = (f32[240]{0:T(256)S(1)}, f32[240]{0:T(256)S(1)}, u32[]{:S(2)}, u32[]{:S(2)}) collective-permute-start(f32[240]{0:T(256)S(1)} %pad_maximum_fusion.2), channel_id=1, source_target_pairs={{0,2},{1,3},{2,0},{3,1},{4,6},{5,7},{6,4},{7,5},{8,10},{9,11},{10,... | collective-permute-start | bytes 2888 | tf_op jit(solution)/shard_map/ppermute | solution.py:336
  145.6 2.2 %copy-start.2 = (f32[240]{0:T(256)}, f32[240]{0:T(256)S(1)}, u32[]{:S(2)}) copy-start(f32[240]{0:T(256)S(1)} %maximum_add_fusion) | copy-start | bytes 2884
Sparse Core Ops, SparseCore 0:
  9.6 70.7 all-gather.1
where the time goes:
time: 156 us; the launch traced here: 155 us
  waiting for transfers between devices  48.3 us (31%)
  Pallas kernels  37.1 us (24%)
  local copies, waits for them, and re-layouts  22.2 us (14%)
  blocking collectives  18.3 us (12%)
  between operations  16.3 us (10%)
  starting transfers between devices  7.15 us (5%)
  other arithmetic  5.23 us (3%)
    all_gather x1, waiting for transfers between devices, gathered(): lax.all_gather(array, 'arc', axis=0, tiled=True, axis_index_groups=gather...  29.8 us
    pallas_call x2, Pallas kernels, fold_call(): pl.pallas_call(functools.partial(fold_kernel, block_rows, width, with_rig...  24.9 us
    all_gather x1, blocking collectives, gathered(): lax.all_gather(array, 'arc', axis=0, tiled=True, axis_index_groups=gather...  18.3 us
    ppermute x3, waiting for transfers between devices, on_device(): vector = lax.ppermute(vector, ('mission', 'arc'), ring(dm, dy))  17.9 us
    pallas_call x1, Pallas kernels, on_device(): pl.pallas_call(projector_kernel, out_shape=jax.ShapeDtypeStruct((block_ro...  12.3 us
    concatenate x2, local copies, waits for them, and re-layouts, fold_call(): jnp.concatenate(picked(lambda block: block * final_rows) + picked(lambda...  6.62 us
    dynamic_slice x1, local copies, waits for them, and re-layouts, picked(): lax.dynamic_slice_in_dim(design_all, start_of(owner), final_rows, 1)  3.82 us
    ppermute x3, starting transfers between devices, on_device(): block = lax.ppermute(block, ('mission', 'arc'), ring(dm, dy))  3.62 us
  transfers between devices with their start and end apart: 7, of which 3 were waited for; matrix products, arithmetic and copies ran while one was open for 11% of the time, Pallas kernels for 16%

commit v1 on v0

--- a/solution.py
+++ b/solution.py
@@ -164,7 +164,7 @@
         ).astype(fold_ref.dtype)
 
 
-def on_device(
+def on_any_mesh(
     design,
     nuisance_design,
     observed,
@@ -341,6 +341,518 @@
     return (fold_total, vector_total[:right_cols], vector_total[right_cols:])
 
 
+TILES = 8
+ARRIVAL = (0, 2, 7, 5, 6, 4, 3, 1)
+SWAPPED = tuple(ARRIVAL.index(tile ^ 1) for tile in ARRIVAL)
+EARLY_Z = 3
+EARLY_X = 5
+
+
+def tile_at(slot, half):
+    tile = ARRIVAL[slot]
+    return tile + half * (1 - 2 * (tile % 2))
+
+
+def slot_of(tile, half):
+    return ARRIVAL.index(tile ^ half)
+
+
+def flip_matrix(size):
+    return (
+        (
+            lax.broadcasted_iota(jnp.int32, (size, size), 0)
+            + lax.broadcasted_iota(jnp.int32, (size, size), 1)
+            == size - 1
+        )
+        .astype(jnp.float32)
+        .astype(jnp.bfloat16)
+    )
+
+
+def weighted_projector(sizes_ref, kinds_ref, weight_ref, nuis_ref, arc_ref, kind_ref, obs_ref):
+    rows = nuis_ref.shape[0]
+    wide = arc_ref.shape[1]
+    lane = lax.broadcasted_iota(jnp.int32, (rows, wide), 1)
+    sub = lax.broadcasted_iota(jnp.int32, (rows, wide), 0)
+    arc_row = arc_ref[...].astype(jnp.float32)
+    kind_row = kind_ref[...]
+    scale_row = jnp.ones((1, wide), jnp.float32)
+    for kind in range(kinds_ref.shape[0]):
+        scale_row = jnp.where(kind_row == kind, 1.0 / kinds_ref[kind], scale_row)
+    arc_col = jnp.sum(jnp.where(lane == sub, arc_row, 0.0), axis=1, keepdims=True)
+    size = jnp.zeros((rows, 1), jnp.int32)
+    for arc in range(sizes_ref.shape[0]):
+        size = jnp.where(arc_col == arc, sizes_ref[arc], size)
+    nuis = nuis_ref[...].astype(jnp.float32)
+    nuis = jnp.where(lax.broadcasted_iota(jnp.int32, nuis.shape, 1) < size, nuis, 0.0)
+    padded = jnp.concatenate(
+        [nuis, jnp.zeros((wide - rows, nuis.shape[1]), jnp.float32)], axis=0
+    )
+    gram = lax.dot_general(
+        nuis.astype(jnp.bfloat16),
+        padded.astype(jnp.bfloat16),
+        (((1,), (1,)), ((), ())),
+        preferred_element_type=jnp.float32,
+    )
+    state = jnp.where(arc_col == arc_row, gram, 0.0)
+    state = state + jnp.where(lane == sub, scale_row, 0.0)
+    for k in range(rows):
+        row = state[k : k + 1, :]
+        col = state[:, k : k + 1]
+        inv = 1.0 / row[:, k : k + 1]
+        scaled_row = row * inv
+        scaled_col = col * inv
+        swept = state - col * scaled_row
+        swept = jnp.where(lane == k, scaled_col, swept)
+        swept = jnp.where(sub == k, scaled_row, swept)
+        state = jnp.where((lane == k) & (sub == k), -inv, swept)
+    inverse = state * -weight_ref[0]
+    reduced_obs = jnp.sum(
+        jnp.where(lane < rows, inverse * obs_ref[...], 0.0), axis=1, keepdims=True
+    )
+    return jnp.where(lane == rows, reduced_obs, inverse).astype(jnp.bfloat16)
+
+
+def normals_kernel(
+    sizes_ref, kinds_ref, weight_ref, design_ref, nuis_ref, arc_ref, kind_ref, obs_ref,
+    fold_ref, vec_out_ref,
+    gath, proj, turned, lhs, right_lhs, part, first_in, second_out, second_in, vec, vec_in,
+    own_sem, z_send, z_recv, x_send, x_recv, r_send, r_recv, d_send, d_recv,
+    one_send, one_recv, two_send, two_recv, v_send, v_recv,
+):
+    rows = nuis_ref.shape[0]
+    tile_cols = gath.shape[2]
+    mission = lax.axis_index("mission")
+    arc = lax.axis_index("arc")
+    core = lax.rem(arc, 2)
+    y = lax.rem(lax.div(arc, 2), 2)
+    near = lax.rem(lax.div(arc, 4), 2)
+    half = lax.div(arc, 8)
+    group = 2 * mission + half
+
+    def device(x=None, zh=None, zl=None, yy=None, c=None):
+        x = mission if x is None else x
+        zh = half if zh is None else zh
+        zl = near if zl is None else zl
+        yy = y if yy is None else yy
+        c = core if c is None else c
+        return (x, ((zh * 2 + zl) * 2 + yy) * 2 + c)
+
+    x_peer = device(x=1 - mission)
+    z_peer = device(zh=1 - half)
+    sibling = device(c=1 - core)
+    y_peer = device(yy=1 - y)
+    near_peer = device(zl=1 - near)
+    cross_peer = device(zl=1 - near, yy=1 - y)
+
+    def block(slot, at):
+        span = pl.ds(at * rows, rows)
+        return proj.at[span] if slot == TILES else gath.at[slot, span]
+
+    def remote(src, dst, send, recv, target):
+        return pltpu.make_async_remote_copy(
+            src_ref=src,
+            dst_ref=dst,
+            send_sem=send,
+            recv_sem=recv,
+            device_id=target,
+            device_id_type=pl.DeviceIdType.MESH,
+        )
+
+    def z_copy(slot):
+        source = slot if slot == TILES else SWAPPED[slot]
+        return remote(block(source, 0), block(slot, 2), z_send.at[slot], z_recv.at[slot], z_peer)
+
+    def x_copy(slot):
+        return remote(block(slot, 0), block(slot, 4), x_send.at[slot], x_recv.at[slot], x_peer)
+
+    def relay(slot):
+        return remote(block(slot, 2), block(slot, 6), r_send.at[slot], r_recv.at[slot], x_peer)
+
+    def share(chip, slot):
+        return remote(
+            block(slot, 2 * chip),
+            block(slot, 2 * chip + 1),
+            d_send.at[chip, slot],
+            d_recv.at[chip, slot],
+            sibling,
+        )
+
+    def own_copy(slot):
+        start = tile_at(slot, half) * tile_cols
+        return pltpu.make_async_copy(
+            design_ref.at[:, pl.ds(pl.multiple_of(start, LANES), tile_cols)],
+            block(slot, 0),
+            own_sem.at[slot],
+        )
+
+    def stage_one(n):
+        if n % 2 == 0:
+            src, target = part.at[n, :, 1 - y], y_peer
+        else:
+            src, target = part.at[n, 1 - near], near_peer
+        return remote(src, first_in.at[n], one_send.at[n], one_recv.at[n], target)
+
+    def stage_two(n):
+        target = near_peer if n % 2 == 0 else y_peer
+        return remote(
+            second_out.at[n], second_in.at[n], two_send.at[n], two_recv.at[n], target
+        )
+
+    def held(n, mine):
+        if n % 2 == 0:
+            at = near if mine else 1 - near
+            return part[n, at, y].astype(jnp.float32) + first_in[n, at].astype(jnp.float32)
+        at = y if mine else 1 - y
+        return part[n, near, at].astype(jnp.float32) + first_in[n, at].astype(jnp.float32)
+
+    def vector_copy(k):
+        target = (y_peer, near_peer, cross_peer)[k]
+        return remote(vec, vec_in.at[k], v_send.at[k], v_recv.at[k], target)
+
+    for slot in range(TILES):
+        own_copy(slot).start()
+    barrier = pltpu.get_barrier_semaphore()
+    peers = (x_peer, z_peer, sibling, y_peer, near_peer, cross_peer)
+    for peer in peers:
+        pl.semaphore_signal(barrier, inc=1, device_id=peer, device_id_type=pl.DeviceIdType.MESH)
+    pl.semaphore_wait(barrier, len(peers))
+    for slot in range(TILES):
+        own_copy(slot).wait()
+    for slot in range(EARLY_Z):
+        z_copy(slot).start()
+    for slot in range(EARLY_X):
+        x_copy(slot).start()
+    for slot in range(TILES):
+        share(0, slot).start()
+
+    proj[pl.ds(0, rows), :] = weighted_projector(
+        sizes_ref, kinds_ref, weight_ref, nuis_ref, arc_ref, kind_ref, obs_ref
+    )
+    z_copy(TILES).start()
+    x_copy(TILES).start()
+    share(0, TILES).start()
+    for slot in range(EARLY_Z, TILES):
+        z_copy(slot).start()
+
+    def from_z(slot):
+        z_copy(slot).wait_recv()
+        relay(slot).start()
+        share(1, slot).start()
+
+    def from_x(slot):
+        x_copy(slot).wait_recv()
+        share(2, slot).start()
+
+    def from_relay(slot):
+        relay(slot).wait_recv()
+        share(3, slot).start()
+
+    def settled(slot):
+        for chip in range(4):
+            share(chip, slot).wait_recv()
+
+    def solved(slot):
+        return jnp.concatenate(
+            [
+                jnp.dot(
+                    proj[pl.ds(at * rows, rows), :][:, :rows],
+                    gath[slot, pl.ds(at * rows, rows), :],
+                    preferred_element_type=jnp.float32,
+                )
+                for at in range(2 * 4)
+            ],
+            axis=0,
+        )
+
+    def make_lhs(mirrored):
+        turned[...] = solved(mission + 2 * mirrored).T.astype(jnp.bfloat16)
+        for to in range(4):
+            start = 2 * rows * to + rows * core
+            if mirrored:
+                start = tile_cols - rows - start
+            picked = turned[pl.ds(pl.multiple_of(start, 16), rows), :]
+            if mirrored:
+                picked = jnp.dot(
+                    flip_matrix(rows), picked, preferred_element_type=jnp.float32
+                ).astype(jnp.bfloat16)
+            lhs[mirrored, pl.ds(to * rows, rows), :] = picked
+
+    def product(mirrored, slot):
+        out = jnp.dot(lhs[mirrored], gath[slot], preferred_element_type=jnp.float32)
+        if not mirrored:
+            return out
+        flip = flip_matrix(LANES)
+        out = out.astype(jnp.bfloat16)
+        return jnp.concatenate(
+            [
+                jnp.dot(out[:, start : start + LANES], flip, preferred_element_type=jnp.float32)
+                for start in range(tile_cols - LANES, -1, -LANES)
+            ],
+            axis=1,
+        )
+
+    def put(n, value):
+        part[n] = value.astype(jnp.bfloat16).reshape(2, 2, rows, tile_cols)
+
+    def either(n, mirror_when, mirror_slot, above_slot):
+        @pl.when(mirror_when)
+        def _():
+            put(n, product(1, mirror_slot))
+
+        @pl.when(jnp.logical_not(mirror_when))
+        def _():
+            put(n, product(0, above_slot))
+
+    def job(n):
+        if n == 0:
+            put(n, product(0, 1 + mission))
+        elif n == 1:
+            put(n, product(0, 2 + mission))
+        elif n == 2:
+            either(n, mission == 1, 2, 3)
+        elif n == 3:
+            local = lax.broadcasted_iota(jnp.int32, (4 * rows, tile_cols), 0)
+            local = lax.div(local, rows) * (2 * rows) + lax.rem(local, rows) + rows * core
+            cols = lax.broadcasted_iota(jnp.int32, (4 * rows, tile_cols), 1)
+            put(n, jnp.where(cols >= local, product(0, mission), product(1, 2 + mission)))
+        elif n == 4:
+            put(n, product(0, 4))
+        elif n == 5:
+            either(n, mission == 1, 4, 5)
+        elif n == 6:
+            put(n, product(0, 6 - mission))
+        else:
+            either(n, half == 1, 4 + mission, 7 - mission)
+        stage_one(n).start()
+
+    def out_tile(n):
+        def above(slot):
+            return tile_at(slot, half)
+
+        def mirror(slot):
+            return TILES - 1 - tile_at(slot, half)
+
+        def by_mission(low, high):
+            return low + mission * (high - low)
+
+        return (
+            lambda: by_mission(above(1), above(2)),
+            lambda: by_mission(above(2), above(3)),
+            lambda: by_mission(above(3), mirror(2)),
+            lambda: group,
+            lambda: above(4),
+            lambda: by_mission(above(5), mirror(4)),
+            lambda: by_mission(above(6), above(5)),
+            lambda: by_mission(
+                above(7) + half * (mirror(4) - above(7)),
+                above(6) + half * (mirror(5) - above(6)),
+            ),
+        )[n]()
+
+    def pass_on(n):
+        stage_one(n).wait_recv()
+        second_out[n] = held(n, False).astype(jnp.bfloat16)
+        stage_two(n).start()
+
+    def finish(n):
+        stage_two(n).wait_recv()
+        start = pl.multiple_of(out_tile(n) * tile_cols, LANES)
+        fold_ref[:, pl.ds(start, tile_cols)] = held(n, True) + second_in[n].astype(jnp.float32)
+
+    def vectors():
+        def by_place(a, b, c, d):
+            return (1 - half) * (a + mission * (b - a)) + half * (c + mission * (d - c))
+
+        low = by_place(
+            slot_of(0, 0), slot_of(4, 0), slot_of(2, 1), slot_of(6, 1)
+        )
+        high = by_place(
+            slot_of(1, 0), slot_of(5, 0), slot_of(3, 1), slot_of(7, 1)
+        )
+        last = by_place(
+            slot_of(4, 0), slot_of(6, 0), slot_of(5, 1), slot_of(7, 1)
+        )
+        lines = [
+            jnp.dot(right_lhs[...], gath[slot], preferred_element_type=jnp.float32)[:1]
+            for slot in (low, high)
+        ]
+        reduced = solved(last).astype(jnp.bfloat16).astype(jnp.float32)
+        lines.append(
+            jnp.sum(gath[last].astype(jnp.float32) * reduced, axis=0, keepdims=True)
+        )
+        at = 0
+        for line in lines:
+            for start in range(0, tile_cols, LANES):
+                vec[at : at + 1, :] = line[:, start : start + LANES]
+                at += 1
+        vec[at:, :] = jnp.zeros((vec.shape[0] - at, LANES), jnp.float32)
+        for k in range(3):
+            vector_copy(k).start()
+
+    from_z(0)
+    from_z(1)
+    for slot in range(EARLY_X, TILES):
+        x_copy(slot).start()
+    for slot in range(3):
+        from_x(slot)
+    from_z(2)
+    from_z(TILES)
+    from_x(TILES)
+    from_relay(0)
+    from_relay(1)
+    from_x(3)
+    from_relay(TILES)
+    from_relay(2)
+    settled(0)
+    settled(1)
+    settled(TILES)
+    make_lhs(0)
+    right_lhs[...] = proj[...].astype(jnp.float32).T.astype(jnp.bfloat16)[rows : rows + 16]
+    settled(2)
+    job(0)
+    from_z(3)
+    from_relay(3)
+    settled(3)
+    job(1)
+    make_lhs(1)
+    job(2)
+    job(3)
+    for slot in range(4, TILES):
+        from_x(slot)
+    from_z(4)
+    from_relay(4)
+    settled(4)
+    job(4)
+    pass_on(0)
+    pass_on(1)
+    from_z(5)
+    from_relay(5)
+    settled(5)
+    job(5)
+    pass_on(2)
+    pass_on(3)
+    finish(0)
+    from_z(6)
+    from_relay(6)
+    settled(6)
+    job(6)
+    pass_on(4)
+    finish(1)
+    finish(2)
+    from_z(7)
+    from_relay(7)
+    settled(7)
+    job(7)
+    vectors()
+    pass_on(5)
+    finish(3)
+    finish(4)
+    pass_on(6)
+    finish(5)
+    pass_on(7)
+    finish(6)
+    total = vec[...]
+    for k in range(3):
+        vector_copy(k).wait_recv()
+        total = total + vec_in[k]
+    vec_out_ref[...] = total
+    finish(7)
+
+    for slot in range(TILES + 1):
+        z_copy(slot).wait_send()
+        x_copy(slot).wait_send()
+        relay(slot).wait_send()
+        for chip in range(4):
+            share(chip, slot).wait_send()
+    for n in range(TILES):
+        stage_one(n).wait_send()
+        stage_two(n).wait_send()
+    for k in range(3):
+        vector_copy(k).wait_send()
+
+
+def on_paired_chips(
+    design,
+    nuisance_design,
+    observed,
+    arc_of_row,
+    nuis_size,
+    weight_index,
+    kind_weight,
+    mission_weight,
+):
+    rows, width_all = design.shape
+    wide = rounded_up(rows + 1, LANES)
+    tile_cols = width_all // TILES
+    stacked = 2 * 4 * rows
+    vec_rows = rounded_up(3 * tile_cols // LANES, 8)
+    vmem = pl.BlockSpec(memory_space=pltpu.VMEM)
+    smem = pl.BlockSpec(memory_space=pltpu.SMEM)
+    dma = pltpu.SemaphoreType.DMA
+    slots = TILES + 1
+
+    def line(array, fill):
+        return jnp.pad(array, (0, wide - rows), constant_values=fill)[None, :]
+
+    fold, vec = pl.pallas_call(
+        normals_kernel,
+        out_shape=(
+            jax.ShapeDtypeStruct((rows, width_all), jnp.float32),
+            jax.ShapeDtypeStruct((vec_rows, LANES), jnp.float32),
+        ),
+        in_specs=[smem, smem, smem, pl.BlockSpec(memory_space=pl.ANY), vmem, vmem, vmem, vmem],
+        out_specs=(vmem, vmem),
+        scratch_shapes=[
+            pltpu.VMEM((TILES, stacked, tile_cols), jnp.bfloat16),
+            pltpu.VMEM((stacked, wide), jnp.bfloat16),
+            pltpu.VMEM((tile_cols, stacked), jnp.bfloat16),
+            pltpu.VMEM((2, 4 * rows, stacked), jnp.bfloat16),
+            pltpu.VMEM((16, stacked), jnp.bfloat16),
+            pltpu.VMEM((TILES, 2, 2, rows, tile_cols), jnp.bfloat16),
+            pltpu.VMEM((TILES, 2, rows, tile_cols), jnp.bfloat16),
+            pltpu.VMEM((TILES, rows, tile_cols), jnp.bfloat16),
+            pltpu.VMEM((TILES, rows, tile_cols), jnp.bfloat16),
+            pltpu.VMEM((vec_rows, LANES), jnp.float32),
+            pltpu.VMEM((3, vec_rows, LANES), jnp.float32),
+            dma((TILES,)),
+            dma((slots,)),
+            dma((slots,)),
+            dma((slots,)),
+            dma((slots,)),
+            dma((slots,)),
+            dma((slots,)),
+            dma((4, slots)),
+            dma((4, slots)),
+            dma((TILES,)),
+            dma((TILES,)),
+            dma((TILES,)),
+            dma((TILES,)),
+            dma((3,)),
+            dma((3,)),
+        ],
+        compiler_params=pltpu.CompilerParams(
+            collective_id=0, has_side_effects=True, vmem_limit_bytes=60 * 2**20
+        ),
+        name="normals",
+    )(
+        nuis_size,
+        kind_weight,
+        mission_weight,
+        design,
+        nuisance_design,
+        line(arc_of_row, -1),
+        line(weight_index, -1),
+        line(observed, 0),
+    )
+    member = lax.rem(lax.axis_index("arc"), 8)
+    right_cols = 2 * rows
+    flat = vec.reshape(-1)
+    right = lax.dynamic_slice_in_dim(flat, member * right_cols, right_cols)
+    tail = lax.dynamic_slice_in_dim(flat, 2 * tile_cols + member * rows, rows)
+    return fold, right, tail
+
+
 def solution(mesh):
     placed = (
         P(("mission", "arc"), None),
@@ -352,6 +864,15 @@
         P(),
         P("mission"),
     )
+
+    def on_device(design, *rest):
+        devices = lax.axis_size("mission") * lax.axis_size("arc")
+        paired = lax.axis_size("mission") == 2 and lax.axis_size("arc") == 16
+        rows, width_all = design.shape
+        if paired and width_all == 2 * devices * rows and rows % 16 == 0 and width_all % (TILES * LANES) == 0:
+            return on_paired_chips(design, *rest)
+        return on_any_mesh(design, *rest)
+
     return jax.shard_map(
         on_device,
         mesh=mesh,

time: 156 us -> 98.2 us (0.63)
  Pallas kernels: 37.1 us -> 88.9 us
  waiting for transfers between devices: 48.3 us -> 0 us
  blocking collectives: 18.3 us -> 0 us
  between operations: 16.3 us -> 1.3 us
  local copies, waits for them, and re-layouts: 22.2 us -> 7.68 us
  starting transfers between devices: 7.15 us -> 0 us
  other arithmetic: 5.23 us -> 0 us
    pallas_call x3 -> x1, Pallas kernels: 37.1 us -> 88.9 us  [on_paired_chips(): pl.pallas_call(normals_kernel, out_shape=(jax.ShapeDtypeStruct((rows, wid...]
    all_gather x1 -> x0, waiting for transfers between devices: 29.8 us -> none  [gathered(): lax.all_gather(array, 'arc', axis=0, tiled=True, axis_index_groups=gather...]
    all_gather x1 -> x0, blocking collectives: 18.3 us -> none  [gathered(): lax.all_gather(array, 'arc', axis=0, tiled=True, axis_index_groups=gather...]
    ppermute x6 -> x0, waiting for transfers between devices: 17.9 us -> none  [the longest x3 17.9 us: on_device(): vector = lax.ppermute(vector, ('mission', 'arc'), ring(dm, dy))]
    ppermute x6 -> x0, starting transfers between devices: 7.12 us -> none  [the longest x3 3.62 us: on_device(): block = lax.ppermute(block, ('mission', 'arc'), ring(dm, dy))]
    concatenate x2 -> x0, local copies, waits for them, and re-layouts: 6.62 us -> none  [fold_call(): jnp.concatenate(picked(lambda block: block * final_rows) + picked(lambda...]
    slice x3 -> x0, local copies, waits for them, and re-layouts: 3.4 us -> none  [the longest x2 2.82 us: on_device(): block = fold[rows]]
    broadcast_in_dim x4 -> x2, local copies, waits for them, and re-layouts: 5.07 us -> 2.36 us  [line(): return jnp.pad(array, (0, wide - rows), constant_values=fill)[None, :]]
  transfers between devices with their start and end apart: 7 -> 0, of which waited for: 3 -> 0; matrix products, arithmetic and copies ran while one was open for 11% -> 0% of each run, Pallas kernels for 16% -> 0%
where the time goes in v1:
time: 98.2 us; the launch traced here: 97.8 us
  Pallas kernels  88.9 us (91%)
  local copies, waits for them, and re-layouts  7.68 us (8%)
  between operations  1.3 us (1%)
    pallas_call x1, Pallas kernels, on_paired_chips(): pl.pallas_call(normals_kernel, out_shape=(jax.ShapeDtypeStruct((rows, wid...  88.9 us
    unnamed x1, local copies, waits for them, and re-layouts  2.72 us
    broadcast_in_dim x2, local copies, waits for them, and re-layouts, line(): return jnp.pad(array, (0, wide - rows), constant_values=fill)[None, :]  2.36 us

profile of v1, /device:TPU:0, one launch (start us, length us, event | category | flops | bytes accessed | tf_op | source)
XLA Modules:
  0.0 97.8 jit_solution(8089462362865208197)
XLA Ops:
  1.3 1.2 %pad_bitcast_fusion.obs_ref = f32[1,128]{1,0:T(1,128)} fusion(f32[80]{0:T(128)} %param.10), kind=kLoop, calls=%fused_computation | loop fusion | bytes 832 | tf_op jit(solution)/shard_map/broadcast_in_dim | solution.py:796
  2.5 1.2 %pad_bitcast_fusion.1 = (s32[1,128]{1,0:T(1,128)}, s32[1,128]{1,0:T(1,128)}) fusion(s32[80]{0:T(128)} %param.13, s32[80]{0:T(128)} %param.11), kind=kLoop, calls=%fused_computation.1 | loop fusion | bytes 1664 | tf_op jit(solution)/shard_map/broadcast_in_dim | solution.py:796
  3.6 88.9 %normals.1 = (f32[80,5120]{1,0:T(8,128)}, f32[16,128]{1,0:T(8,128)}) custom-call(s32[2]{0:T(128)} %sizes_ref.1, f32[8]{0:T(128)} %kinds_ref.1, f32[1]{0:T(128)S(6)} %copy.12.weight_ref, bf16[80,5120]{1,0:T(8,128)(2,1)} %design_ref.1, bf16[80,128]{1,0:T(8,128)(2,1)} %nuis_ref.1, s32[1,128]{1,0:T(1,128)} %get-tuple-element.8.arc_ref, ...), custom_call_target="tpu_custom_call" | custom-call | tf_op jit(solution)/shard_map/normals/pallas_call | solution.py:798
  92.5 1.3 %dynamic_slice.7 = f32[80]{0:T(128)} dynamic-slice(f32[2048]{0:T(1024)} %bitcast.7, s32[]{:T(128)S(6)} %select_n.7), dynamic_slice_sizes={80} | dynamic-slice | bytes 644 | tf_op jit(solution)/shard_map/dynamic_slice | solution.py:852
  93.8 1.3 %dynamic_slice.6 = f32[160]{0:T(256)} dynamic-slice(f32[2048]{0:T(1024)} %bitcast.8, s32[]{:T(128)S(6)} %select_n.6), dynamic_slice_sizes={160} | dynamic-slice | bytes 1284 | tf_op jit(solution)/shard_map/dynamic_slice | solution.py:851
  95.1 2.7 %copy.13 = f32[80,5120]{1,0:T(8,128)} copy(f32[80,5120]{1,0:T(8,128)} %get-tuple-element.12) | data formatting | bytes 3276800

commit v2 on v1

--- a/solution.py
+++ b/solution.py
@@ -343,14 +343,22 @@
 
 TILES = 8
 ARRIVAL = (0, 2, 7, 5, 6, 4, 3, 1)
+Y_FIRST = (True, True, True, True, True, False, True, False)
 SWAPPED = tuple(ARRIVAL.index(tile ^ 1) for tile in ARRIVAL)
-EARLY_Z = 3
-EARLY_X = 5
 
 
 def tile_at(slot, half):
     tile = ARRIVAL[slot]
     return tile + half * (1 - 2 * (tile % 2))
+
+
+def scoped(step):
+    @functools.wraps(step)
+    def run(*at):
+        with jax.named_scope("_".join([step.__name__, *map(str, at[:1])])):
+            return step(*at)
+
+    return run
 
 
 def slot_of(tile, half):
@@ -369,13 +377,18 @@
     )
 
 
-def weighted_projector(sizes_ref, kinds_ref, weight_ref, nuis_ref, arc_ref, kind_ref, obs_ref):
+def in_line(ref, wide, fill):
+    line = ref[...].reshape(1, -1)
+    return jnp.concatenate([line, jnp.full((1, wide - line.shape[1]), fill, line.dtype)], axis=1)
+
+
+def projector_start(sizes_ref, kinds_ref, nuis_ref, arc_ref, kind_ref):
     rows = nuis_ref.shape[0]
-    wide = arc_ref.shape[1]
+    wide = rounded_up(rows + 1, LANES)
     lane = lax.broadcasted_iota(jnp.int32, (rows, wide), 1)
     sub = lax.broadcasted_iota(jnp.int32, (rows, wide), 0)
-    arc_row = arc_ref[...].astype(jnp.float32)
-    kind_row = kind_ref[...]
+    arc_row = in_line(arc_ref, wide, -1).astype(jnp.float32)
+    kind_row = in_line(kind_ref, wide, -1)
     scale_row = jnp.ones((1, wide), jnp.float32)
     for kind in range(kinds_ref.shape[0]):
         scale_row = jnp.where(kind_row == kind, 1.0 / kinds_ref[kind], scale_row)
@@ -395,28 +408,55 @@
         preferred_element_type=jnp.float32,
     )
     state = jnp.where(arc_col == arc_row, gram, 0.0)
-    state = state + jnp.where(lane == sub, scale_row, 0.0)
-    for k in range(rows):
-        row = state[k : k + 1, :]
-        col = state[:, k : k + 1]
+    return state + jnp.where(lane == sub, scale_row, 0.0)
+
+
+def eliminate(state, first, last):
+    rows, wide = state.shape
+    deep = 8
+    lane = lax.broadcasted_iota(jnp.int32, (deep, wide), 1)
+    sub = lax.broadcasted_iota(jnp.int32, (deep, wide), 0)
+    bands = [state[at : at + deep] for at in range(0, rows, deep)]
+    for k in range(first, last):
+        at, off = k // deep, k % deep
+        row = bands[at][off : off + 1, :]
         inv = 1.0 / row[:, k : k + 1]
-        scaled_row = row * inv
-        scaled_col = col * inv
-        swept = state - col * scaled_row
-        swept = jnp.where(lane == k, scaled_col, swept)
-        swept = jnp.where(sub == k, scaled_row, swept)
-        state = jnp.where((lane == k) & (sub == k), -inv, swept)
-    inverse = state * -weight_ref[0]
+        scaled = jnp.where(lane[:1] == k, inv, row * inv)
+        for band in range(at, rows // deep):
+            col = bands[band][:, k : k + 1]
+            hit = lane == k
+            if band == at:
+                if off == deep - 1:
+                    continue
+                col = jnp.where(sub[:, :1] > off, col, 0.0)
+                hit = hit & (sub > off)
+            bands[band] = jnp.where(hit, 0.0, bands[band]) - col * scaled
+    return jnp.concatenate(bands, axis=0)
+
+
+def projector_end(state, weight_ref, obs_ref):
+    rows = state.shape[0]
+    lane = lax.broadcasted_iota(jnp.int32, state.shape, 1)
+    sub = lax.broadcasted_iota(jnp.int32, state.shape, 0)
+    pivot = jnp.sum(jnp.where(lane == sub, state, 0.0), axis=1, keepdims=True)
+    factor = jnp.where(lane < sub, state, jnp.where(lane == sub, 1.0, 0.0))
+    inverse = lax.dot_general(
+        factor,
+        factor * (weight_ref[0] / pivot),
+        (((0,), (0,)), ((), ())),
+        precision=lax.Precision.HIGHEST,
+        preferred_element_type=jnp.float32,
+    )[:rows]
     reduced_obs = jnp.sum(
-        jnp.where(lane < rows, inverse * obs_ref[...], 0.0), axis=1, keepdims=True
+        jnp.where(lane < rows, inverse * in_line(obs_ref, lane.shape[1], 0), 0.0), axis=1, keepdims=True
     )
     return jnp.where(lane == rows, reduced_obs, inverse).astype(jnp.bfloat16)
 
 
 def normals_kernel(
     sizes_ref, kinds_ref, weight_ref, design_ref, nuis_ref, arc_ref, kind_ref, obs_ref,
-    fold_ref, vec_out_ref,
-    gath, proj, turned, lhs, right_lhs, part, first_in, second_out, second_in, vec, vec_in,
+    kept_ref, sent_ref, right_ref, tail_ref,
+    gath, proj, state_ref, turned, lhs, right_lhs, part, first_in, second_out, second_in, vec, vec_in,
     own_sem, z_send, z_recv, x_send, x_recv, r_send, r_recv, d_send, d_recv,
     one_send, one_recv, two_send, two_recv, v_send, v_recv,
 ):
@@ -487,20 +527,20 @@
         )
 
     def stage_one(n):
-        if n % 2 == 0:
+        if Y_FIRST[n]:
             src, target = part.at[n, :, 1 - y], y_peer
         else:
             src, target = part.at[n, 1 - near], near_peer
         return remote(src, first_in.at[n], one_send.at[n], one_recv.at[n], target)
 
     def stage_two(n):
-        target = near_peer if n % 2 == 0 else y_peer
+        target = near_peer if Y_FIRST[n] else y_peer
         return remote(
             second_out.at[n], second_in.at[n], two_send.at[n], two_recv.at[n], target
         )
 
     def held(n, mine):
-        if n % 2 == 0:
+        if Y_FIRST[n]:
             at = near if mine else 1 - near
             return part[n, at, y].astype(jnp.float32) + first_in[n, at].astype(jnp.float32)
         at = y if mine else 1 - y
@@ -508,7 +548,8 @@
 
     def vector_copy(k):
         target = (y_peer, near_peer, cross_peer)[k]
-        return remote(vec, vec_in.at[k], v_send.at[k], v_recv.at[k], target)
+        to = (2 * near + 1 - y, 2 * (1 - near) + y, 2 * (1 - near) + 1 - y)[k]
+        return remote(vec.at[to], vec_in.at[k], v_send.at[k], v_recv.at[k], target)
 
     for slot in range(TILES):
         own_copy(slot).start()
@@ -516,38 +557,43 @@
     peers = (x_peer, z_peer, sibling, y_peer, near_peer, cross_peer)
     for peer in peers:
         pl.semaphore_signal(barrier, inc=1, device_id=peer, device_id_type=pl.DeviceIdType.MESH)
+    step = rows // 16
+    ends = near == half
+
+    def apart(work):
+        pl.when(arc >= 0)(work)
+
+    def sweep(first, last):
+        @apart
+        def _():
+            with jax.named_scope('elim'):
+                state_ref[...] = eliminate(state_ref[...], first, last)
+
+    @apart
+    def _():
+        state = projector_start(sizes_ref, kinds_ref, nuis_ref, arc_ref, kind_ref)
+        state_ref[...] = eliminate(state, 0, 2 * step)
+
     pl.semaphore_wait(barrier, len(peers))
     for slot in range(TILES):
         own_copy(slot).wait()
-    for slot in range(EARLY_Z):
-        z_copy(slot).start()
-    for slot in range(EARLY_X):
-        x_copy(slot).start()
-    for slot in range(TILES):
-        share(0, slot).start()
-
-    proj[pl.ds(0, rows), :] = weighted_projector(
-        sizes_ref, kinds_ref, weight_ref, nuis_ref, arc_ref, kind_ref, obs_ref
-    )
-    z_copy(TILES).start()
-    x_copy(TILES).start()
-    share(0, TILES).start()
-    for slot in range(EARLY_Z, TILES):
-        z_copy(slot).start()
-
+    @scoped
     def from_z(slot):
         z_copy(slot).wait_recv()
         relay(slot).start()
         share(1, slot).start()
 
+    @scoped
     def from_x(slot):
         x_copy(slot).wait_recv()
         share(2, slot).start()
 
+    @scoped
     def from_relay(slot):
         relay(slot).wait_recv()
         share(3, slot).start()
 
+    @scoped
     def settled(slot):
         for chip in range(4):
             share(chip, slot).wait_recv()
@@ -565,6 +611,7 @@
             axis=0,
         )
 
+    @scoped
     def make_lhs(mirrored):
         turned[...] = solved(mission + 2 * mirrored).T.astype(jnp.bfloat16)
         for to in range(4):
@@ -595,71 +642,142 @@
     def put(n, value):
         part[n] = value.astype(jnp.bfloat16).reshape(2, 2, rows, tile_cols)
 
-    def either(n, mirror_when, mirror_slot, above_slot):
-        @pl.when(mirror_when)
-        def _():
-            put(n, product(1, mirror_slot))
-
-        @pl.when(jnp.logical_not(mirror_when))
-        def _():
-            put(n, product(0, above_slot))
-
-    def job(n):
-        if n == 0:
-            put(n, product(0, 1 + mission))
-        elif n == 1:
-            put(n, product(0, 2 + mission))
-        elif n == 2:
-            either(n, mission == 1, 2, 3)
-        elif n == 3:
-            local = lax.broadcasted_iota(jnp.int32, (4 * rows, tile_cols), 0)
-            local = lax.div(local, rows) * (2 * rows) + lax.rem(local, rows) + rows * core
-            cols = lax.broadcasted_iota(jnp.int32, (4 * rows, tile_cols), 1)
-            put(n, jnp.where(cols >= local, product(0, mission), product(1, 2 + mission)))
-        elif n == 4:
-            put(n, product(0, 4))
-        elif n == 5:
-            either(n, mission == 1, 4, 5)
-        elif n == 6:
-            put(n, product(0, 6 - mission))
+    def diagonal(n):
+        local = lax.broadcasted_iota(jnp.int32, (4 * rows, tile_cols), 0)
+        local = lax.div(local, rows) * (2 * rows) + lax.rem(local, rows) + rows * core
+        cols = lax.broadcasted_iota(jnp.int32, (4 * rows, tile_cols), 1)
+        put(n, jnp.where(cols >= local, product(0, mission), product(1, 2 + mission)))
+        stage_one(n).start()
+
+    def above(n, slot):
+        put(n, product(0, slot))
+        stage_one(n).start()
+
+    def mirrored(n, slot):
+        put(n, product(1, slot))
+        stage_one(n).start()
+
+    def low(work):
+        pl.when(mission == 0)(work)
+
+    def high(work):
+        pl.when(mission == 1)(work)
+
+    def on(x, zh):
+        return pl.when(jnp.logical_and(mission == x, half == zh))
+
+    @scoped
+    def jobs_at(slot):
+        if slot == 1:
+
+            @low
+            def _():
+                above(0, 1)
+
+        elif slot == 2:
+
+            @low
+            def _():
+                above(1, 2)
+                make_lhs(1)
+                diagonal(2)
+
+            @high
+            def _():
+                above(0, 2)
+
+        elif slot == 3:
+
+            @low
+            def _():
+                above(3, 3)
+
+            @high
+            def _():
+                above(1, 3)
+                make_lhs(1)
+                diagonal(2)
+                mirrored(3, 2)
+
+        elif slot == 4:
+            above(4, 4)
+
+            @high
+            def _():
+                mirrored(5, 4)
+
+            @on(0, 1)
+            def _():
+                mirrored(7, 4)
+
+        elif slot == 5:
+
+            @low
+            def _():
+                above(5, 5)
+
+            @high
+            def _():
+                above(6, 5)
+
+            @on(1, 1)
+            def _():
+                mirrored(7, 5)
+
+        elif slot == 6:
+
+            @low
+            def _():
+                above(6, 6)
+
+            @on(1, 0)
+            def _():
+                above(7, 6)
+
         else:
-            either(n, half == 1, 4 + mission, 7 - mission)
-        stage_one(n).start()
+
+            @on(0, 0)
+            def _():
+                above(7, 7)
 
     def out_tile(n):
-        def above(slot):
+        def upper(slot):
             return tile_at(slot, half)
 
-        def mirror(slot):
+        def lower(slot):
             return TILES - 1 - tile_at(slot, half)
 
         def by_mission(low, high):
             return low + mission * (high - low)
 
         return (
-            lambda: by_mission(above(1), above(2)),
-            lambda: by_mission(above(2), above(3)),
-            lambda: by_mission(above(3), mirror(2)),
+            lambda: by_mission(upper(1), upper(2)),
+            lambda: by_mission(upper(2), upper(3)),
             lambda: group,
-            lambda: above(4),
-            lambda: by_mission(above(5), mirror(4)),
-            lambda: by_mission(above(6), above(5)),
+            lambda: by_mission(upper(3), lower(2)),
+            lambda: upper(4),
+            lambda: by_mission(upper(5), lower(4)),
+            lambda: by_mission(upper(6), upper(5)),
             lambda: by_mission(
-                above(7) + half * (mirror(4) - above(7)),
-                above(6) + half * (mirror(5) - above(6)),
+                upper(7) + half * (lower(4) - upper(7)),
+                upper(6) + half * (lower(5) - upper(6)),
             ),
         )[n]()
 
+    @scoped
     def pass_on(n):
         stage_one(n).wait_recv()
         second_out[n] = held(n, False).astype(jnp.bfloat16)
         stage_two(n).start()
 
+    @scoped
     def finish(n):
         stage_two(n).wait_recv()
         start = pl.multiple_of(out_tile(n) * tile_cols, LANES)
-        fold_ref[:, pl.ds(start, tile_cols)] = held(n, True) + second_in[n].astype(jnp.float32)
-
+        kept_ref[:, pl.ds(start, tile_cols)] = held(n, True).astype(jnp.bfloat16)
+        sent_ref[:, pl.ds(start, tile_cols)] = second_in[n]
+
+    @scoped
     def vectors():
         def by_place(a, b, c, d):
             return (1 - half) * (a + mission * (b - a)) + half * (c + mission * (d - c))
@@ -681,86 +799,141 @@
         lines.append(
             jnp.sum(gath[last].astype(jnp.float32) * reduced, axis=0, keepdims=True)
         )
-        at = 0
-        for line in lines:
-            for start in range(0, tile_cols, LANES):
-                vec[at : at + 1, :] = line[:, start : start + LANES]
-                at += 1
-        vec[at:, :] = jnp.zeros((vec.shape[0] - at, LANES), jnp.float32)
+        right = jnp.concatenate(lines[:2], axis=1)
+        for to in range(4):
+            parts = []
+            for line, width in ((right, 2 * rows), (lines[2], rows)):
+                even, odd = (
+                    line[:, at * width : (at + 1) * width] for at in (2 * to, 2 * to + 1)
+                )
+                parts.append(jnp.where(core == 0, even, odd))
+            parts.append(jnp.zeros((1, vec.shape[2] - 3 * rows), jnp.float32))
+            vec[to, :1, :] = jnp.concatenate(parts, axis=1)
         for k in range(3):
             vector_copy(k).start()
 
+    @scoped
+    def next_z(slot):
+        z_copy(slot).wait_send()
+        if slot + 2 < TILES:
+
+            @pl.when(jnp.logical_not(ends))
+            def _():
+                z_copy(slot + 2).start()
+
+        early = (2,) if slot == 1 else (3, 4) if slot == 2 else (slot + 2,)
+        early = tuple(at for at in early if 2 <= at < TILES) if slot else ()
+        if early:
+
+            @pl.when(ends)
+            def _():
+                for at in early:
+                    z_copy(at).start()
+
+    def next_x(slot):
+        x_copy(slot).start()
+
+    z_copy(0).start()
+    x_copy(0).start()
+    z_copy(1).start()
+    x_copy(1).start()
+    x_copy(2).start()
+    for slot in range(TILES):
+        share(0, slot).start()
+    sweep(2 * step, rows)
+
+    @apart
+    @scoped
+    def project():
+        proj[pl.ds(0, rows), :] = projector_end(state_ref[...], weight_ref, obs_ref)
+
+    z_copy(TILES).start()
+    x_copy(TILES).start()
+    share(0, TILES).start()
+    from_x(0)
+    from_x(1)
     from_z(0)
+    next_z(0)
+    from_x(TILES)
     from_z(1)
-    for slot in range(EARLY_X, TILES):
-        x_copy(slot).start()
-    for slot in range(3):
-        from_x(slot)
+    next_x(3)
+    next_z(1)
+    from_relay(0)
+    from_z(TILES)
+    from_x(2)
+    next_x(4)
+    from_relay(1)
+    settled(0)
     from_z(2)
-    from_z(TILES)
-    from_x(TILES)
-    from_relay(0)
-    from_relay(1)
-    from_x(3)
+    next_z(2)
     from_relay(TILES)
-    from_relay(2)
-    settled(0)
     settled(1)
     settled(TILES)
     make_lhs(0)
+    jobs_at(1)
     right_lhs[...] = proj[...].astype(jnp.float32).T.astype(jnp.bfloat16)[rows : rows + 16]
+    from_x(3)
+    from_relay(2)
+    from_z(3)
+    next_z(3)
+    next_x(5)
     settled(2)
-    job(0)
-    from_z(3)
+    jobs_at(2)
+    from_x(4)
     from_relay(3)
+    from_z(4)
+    next_z(4)
+    next_x(6)
     settled(3)
-    job(1)
-    make_lhs(1)
-    job(2)
-    job(3)
-    for slot in range(4, TILES):
-        from_x(slot)
-    from_z(4)
+    jobs_at(3)
+    pass_on(0)
+    from_x(5)
     from_relay(4)
+    from_z(5)
+    next_z(5)
+    next_x(7)
     settled(4)
-    job(4)
-    pass_on(0)
+    jobs_at(4)
     pass_on(1)
-    from_z(5)
+    from_x(6)
     from_relay(5)
+    from_z(6)
+    next_z(6)
     settled(5)
-    job(5)
+    jobs_at(5)
     pass_on(2)
     pass_on(3)
     finish(0)
-    from_z(6)
+    from_x(7)
     from_relay(6)
+    from_z(7)
+    next_z(7)
     settled(6)
-    job(6)
+    jobs_at(6)
     pass_on(4)
     finish(1)
-    finish(2)
-    from_z(7)
     from_relay(7)
     settled(7)
-    job(7)
+    jobs_at(7)
     vectors()
     pass_on(5)
+    finish(2)
     finish(3)
+    pass_on(6)
     finish(4)
-    pass_on(6)
     finish(5)
     pass_on(7)
     finish(6)
-    total = vec[...]
+    total = vec[2 * near + y, :1, :]
     for k in range(3):
         vector_copy(k).wait_recv()
-        total = total + vec_in[k]
-    vec_out_ref[...] = total
+        total = total + vec_in[k, :1, :]
+    right_ref[...] = total[:, : 2 * rows]
+    tail_ref[...] = total[:, 2 * rows : 3 * rows]
     finish(7)
 
+    z_copy(TILES).wait_send()
     for slot in range(TILES + 1):
-        z_copy(slot).wait_send()
         x_copy(slot).wait_send()
         relay(slot).wait_send()
         for chip in range(4):
@@ -786,26 +959,26 @@
     wide = rounded_up(rows + 1, LANES)
     tile_cols = width_all // TILES
     stacked = 2 * 4 * rows
-    vec_rows = rounded_up(3 * tile_cols // LANES, 8)
+    vec_cols = rounded_up(3 * rows, LANES)
     vmem = pl.BlockSpec(memory_space=pltpu.VMEM)
     smem = pl.BlockSpec(memory_space=pltpu.SMEM)
     dma = pltpu.SemaphoreType.DMA
     slots = TILES + 1
 
-    def line(array, fill):
-        return jnp.pad(array, (0, wide - rows), constant_values=fill)[None, :]
-
-    fold, vec = pl.pallas_call(
+    kept, sent, right, tail = pl.pallas_call(
         normals_kernel,
         out_shape=(
-            jax.ShapeDtypeStruct((rows, width_all), jnp.float32),
-            jax.ShapeDtypeStruct((vec_rows, LANES), jnp.float32),
+            jax.ShapeDtypeStruct((rows, width_all), jnp.bfloat16),
+            jax.ShapeDtypeStruct((rows, width_all), jnp.bfloat16),
+            jax.ShapeDtypeStruct((1, 2 * rows), jnp.float32),
+            jax.ShapeDtypeStruct((1, rows), jnp.float32),
         ),
         in_specs=[smem, smem, smem, pl.BlockSpec(memory_space=pl.ANY), vmem, vmem, vmem, vmem],
-        out_specs=(vmem, vmem),
+        out_specs=(vmem, vmem, vmem, vmem),
         scratch_shapes=[
             pltpu.VMEM((TILES, stacked, tile_cols), jnp.bfloat16),
             pltpu.VMEM((stacked, wide), jnp.bfloat16),
+            pltpu.VMEM((rows, wide), jnp.float32),
             pltpu.VMEM((tile_cols, stacked), jnp.bfloat16),
             pltpu.VMEM((2, 4 * rows, stacked), jnp.bfloat16),
             pltpu.VMEM((16, stacked), jnp.bfloat16),
@@ -813,8 +986,8 @@
             pltpu.VMEM((TILES, 2, rows, tile_cols), jnp.bfloat16),
             pltpu.VMEM((TILES, rows, tile_cols), jnp.bfloat16),
             pltpu.VMEM((TILES, rows, tile_cols), jnp.bfloat16),
-            pltpu.VMEM((vec_rows, LANES), jnp.float32),
-            pltpu.VMEM((3, vec_rows, LANES), jnp.float32),
+            pltpu.VMEM((4, 8, vec_cols), jnp.float32),
+            pltpu.VMEM((3, 8, vec_cols), jnp.float32),
             dma((TILES,)),
             dma((slots,)),
             dma((slots,)),
@@ -841,16 +1014,12 @@
         mission_weight,
         design,
         nuisance_design,
-        line(arc_of_row, -1),
-        line(weight_index, -1),
-        line(observed, 0),
+        arc_of_row,
+        weight_index,
+        observed,
     )
-    member = lax.rem(lax.axis_index("arc"), 8)
-    right_cols = 2 * rows
-    flat = vec.reshape(-1)
-    right = lax.dynamic_slice_in_dim(flat, member * right_cols, right_cols)
-    tail = lax.dynamic_slice_in_dim(flat, 2 * tile_cols + member * rows, rows)
-    return fold, right, tail
+    fold = kept.astype(jnp.float32) + sent.astype(jnp.float32)
+    return fold, right.reshape(-1), tail.reshape(-1)
 
 
 def solution(mesh):

time: 98.2 us -> 72.4 us (0.74)
  Pallas kernels: 88.9 us -> 66.4 us
  local copies, waits for them, and re-layouts: 7.68 us -> 1.08 us
  other arithmetic: 0 us -> 2.74 us
    pallas_call x1, Pallas kernels: 88.9 us -> 66.4 us  [on_paired_chips(): pl.pallas_call(normals_kernel, out_shape=(jax.ShapeDtypeStruct((rows, wid...]
    add x0 -> x1, other arithmetic: none -> 2.74 us  [on_paired_chips(): fold = kept.astype(jnp.float32) + sent.astype(jnp.float32)]
    dynamic_slice x2 -> x0, local copies, waits for them, and re-layouts: 2.6 us -> none  [the longest x1 1.33 us: on_paired_chips(): right = lax.dynamic_slice_in_dim(flat, member * right_cols, right_cols)]
    broadcast_in_dim x2 -> x0, local copies, waits for them, and re-layouts: 2.36 us -> none  [line(): return jnp.pad(array, (0, wide - rows), constant_values=fill)[None, :]]
    unnamed x1 -> x6, local copies, waits for them, and re-layouts: 2.72 us -> 1.08 us
where the time goes in v2:
time: 72.4 us; the launch traced here: 71.5 us
  Pallas kernels  66.4 us (92%)
  other arithmetic  2.74 us (4%)
  between operations  1.31 us (2%)
  local copies, waits for them, and re-layouts  1.08 us (1%)
    pallas_call x1, Pallas kernels, on_paired_chips(): pl.pallas_call(normals_kernel, out_shape=(jax.ShapeDtypeStruct((rows, wid...  66.4 us
    add x1, other arithmetic, on_paired_chips(): fold = kept.astype(jnp.float32) + sent.astype(jnp.float32)  2.74 us

profile of v2, /device:TPU:0, one launch (start us, length us, event | category | flops | bytes accessed | tf_op | source)
XLA Modules:
  0.0 71.5 jit_solution(4780055404610148794)
XLA Ops:
  1.3 66.4 %normals.1 = (bf16[80,5120]{1,0:T(8,128)(2,1)}, bf16[80,5120]{1,0:T(8,128)(2,1)}, f32[1,160]{1,0:T(1,128)}, f32[1,80]{1,0:T(1,128)}) custom-call(s32[2]{0:T(128)} %sizes_ref.1, f32[8]{0:T(128)} %kinds_ref.1, f32[1]{0:T(128)S(6)} %copy.13.weight_ref, bf16[80,5120]{1,0:T(8,128)(2,1)} %design_ref.1, bf16[80,128]{1,0:T(8,128)(2,1)} %nuis_ref.1, s32[80]{0:T(128)} %arc_ref.1, ...), custom_call_target="tpu_custom_call" | custom-call | tf_op jit(solution)/shard_map/normals/pallas_call | solution.py:968
  67.7 0.0 copy-start
  67.7 0.0 copy-start.1
  67.7 2.7 %convert_add_fusion = f32[80,5120]{1,0:T(8,128)} fusion(bf16[80,5120]{1,0:T(8,128)(2,1)} %get-tuple-element.8, bf16[80,5120]{1,0:T(8,128)(2,1)} %get-tuple-element.7), kind=kLoop, calls=%fused_computation | loop fusion | flops 1228800 | bytes 3276800 | tf_op jit(solution)/shard_map/add | solution.py:1021
  70.5 0.0 copy-done
  70.5 0.6 copy.14
  71.0 0.0 copy-done.1
  71.0 0.5 copy.15
Async XLA Ops:
  67.7 2.8 %copy-start = (f32[1,160]{1,0:T(1,128)S(1)}, f32[1,160]{1,0:T(1,128)}, u32[]{:S(2)}) copy-start(f32[1,160]{1,0:T(1,128)} %get-tuple-element.9) | copy-start | bytes 1924
  67.7 3.3 %copy-start.1 = (f32[1,80]{1,0:T(1,128)S(1)}, f32[1,80]{1,0:T(1,128)}, u32[]{:S(2)}) copy-start(f32[1,80]{1,0:T(1,128)} %get-tuple-element.10) | copy-start | bytes 964

commit v3 on v0

--- a/solution.py
+++ b/solution.py
@@ -164,7 +164,7 @@
         ).astype(fold_ref.dtype)
 
 
-def on_device(
+def on_any_mesh(
     design,
     nuisance_design,
     observed,
@@ -341,6 +341,903 @@
     return (fold_total, vector_total[:right_cols], vector_total[right_cols:])
 
 
+TILES = 8
+ARRIVAL = (0, 2, 5, 7, 6, 4, 3, 1)
+Y_FIRST = (
+    (True, False, True, False, True, True, False, True,),
+    (True, False, True, False, True, True, False, True,),
+)
+STRAIGHT = ((), ())
+SWAPPED = tuple(ARRIVAL.index(tile ^ 1) for tile in ARRIVAL)
+
+
+def tile_at(slot, half):
+    tile = ARRIVAL[slot]
+    return tile + half * (1 - 2 * (tile % 2))
+
+
+def scoped(step):
+    @functools.wraps(step)
+    def run(*at):
+        with jax.named_scope("_".join([step.__name__, *map(str, at[:1])])):
+            return step(*at)
+
+    return run
+
+
+def slot_of(tile, half):
+    return ARRIVAL.index(tile ^ half)
+
+
+def flip_matrix(size):
+    return (
+        (
+            lax.broadcasted_iota(jnp.int32, (size, size), 0)
+            + lax.broadcasted_iota(jnp.int32, (size, size), 1)
+            == size - 1
+        )
+        .astype(jnp.float32)
+        .astype(jnp.bfloat16)
+    )
+
+
+def in_line(ref, wide, fill):
+    line = ref[...].reshape(1, -1)
+    return jnp.concatenate([line, jnp.full((1, wide - line.shape[1]), fill, line.dtype)], axis=1)
+
+
+def projector_start(sizes_ref, kinds_ref, nuis_ref, arc_ref, kind_ref):
+    rows = nuis_ref.shape[0]
+    wide = rounded_up(rows + 1, LANES)
+    lane = lax.broadcasted_iota(jnp.int32, (rows, wide), 1)
+    sub = lax.broadcasted_iota(jnp.int32, (rows, wide), 0)
+    arc_row = in_line(arc_ref, wide, -1).astype(jnp.float32)
+    kind_row = in_line(kind_ref, wide, -1)
+    scale_row = jnp.ones((1, wide), jnp.float32)
+    for kind in range(kinds_ref.shape[0]):
+        scale_row = jnp.where(kind_row == kind, 1.0 / kinds_ref[kind], scale_row)
+    arc_col = jnp.sum(jnp.where(lane == sub, arc_row, 0.0), axis=1, keepdims=True)
+    size = jnp.zeros((rows, 1), jnp.int32)
+    for arc in range(sizes_ref.shape[0]):
+        size = jnp.where(arc_col == arc, sizes_ref[arc], size)
+    nuis = nuis_ref[...].astype(jnp.float32)
+    nuis = jnp.where(lax.broadcasted_iota(jnp.int32, nuis.shape, 1) < size, nuis, 0.0)
+    padded = jnp.concatenate(
+        [nuis, jnp.zeros((wide - rows, nuis.shape[1]), jnp.float32)], axis=0
+    )
+    gram = lax.dot_general(
+        nuis.astype(jnp.bfloat16),
+        padded.astype(jnp.bfloat16),
+        (((1,), (1,)), ((), ())),
+        preferred_element_type=jnp.float32,
+    )
+    state = jnp.where(arc_col == arc_row, gram, 0.0)
+    return state + jnp.where(lane == sub, scale_row, 0.0)
+
+
+def eliminate(state, first, last):
+    rows, wide = state.shape
+    deep = 8
+    lane = lax.broadcasted_iota(jnp.int32, (deep, wide), 1)
+    sub = lax.broadcasted_iota(jnp.int32, (deep, wide), 0)
+    bands = [state[at : at + deep] for at in range(0, rows, deep)]
+    for k in range(first, last):
+        at, off = k // deep, k % deep
+        row = bands[at][off : off + 1, :]
+        inv = 1.0 / row[:, k : k + 1]
+        scaled = jnp.where(lane[:1] == k, inv, row * inv)
+        for band in range(at, rows // deep):
+            col = bands[band][:, k : k + 1]
+            hit = lane == k
+            if band == at:
+                if off == deep - 1:
+                    continue
+                col = jnp.where(sub[:, :1] > off, col, 0.0)
+                hit = hit & (sub > off)
+            bands[band] = jnp.where(hit, 0.0, bands[band]) - col * scaled
+    return jnp.concatenate(bands, axis=0)
+
+
+def projector_end(state, weight_ref, obs_ref):
+    rows = state.shape[0]
+    lane = lax.broadcasted_iota(jnp.int32, state.shape, 1)
+    sub = lax.broadcasted_iota(jnp.int32, state.shape, 0)
+    pivot = jnp.sum(jnp.where(lane == sub, state, 0.0), axis=1, keepdims=True)
+    factor = jnp.where(lane < sub, state, jnp.where(lane == sub, 1.0, 0.0))
+    inverse = lax.dot_general(
+        factor,
+        factor * (weight_ref[...].reshape(1, 1) / pivot),
+        (((0,), (0,)), ((), ())),
+        precision=lax.Precision.HIGHEST,
+        preferred_element_type=jnp.float32,
+    )[:rows]
+    reduced_obs = jnp.sum(
+        jnp.where(lane < rows, inverse * in_line(obs_ref, lane.shape[1], 0), 0.0), axis=1, keepdims=True
+    )
+    return jnp.where(lane == rows, reduced_obs, inverse).astype(jnp.bfloat16)
+
+
+def normals_kernel(
+    sizes_ref, kinds_ref, weight_ref, design_ref, nuis_ref, arc_ref, kind_ref, obs_ref,
+    fold_ref, right_ref, tail_ref,
+    gath, proj, state_ref, turned, lhs, right_lhs, part, first_in, second_out, second_in, vec, vec_in,
+    own_sem, z_send, z_recv, x_send, x_recv, r_send, r_recv, d_send, d_recv,
+    one_send, one_recv, two_send, two_recv, s_send, s_recv, v_send, v_recv,
+):
+    rows = nuis_ref.shape[0]
+    tile_cols = gath.shape[2]
+    mission = lax.axis_index("mission")
+    arc = lax.axis_index("arc")
+    core = lax.rem(arc, 2)
+    y = lax.rem(lax.div(arc, 2), 2)
+    near = lax.rem(lax.div(arc, 4), 2)
+    half = lax.div(arc, 8)
+    group = 2 * mission + half
+
+    def device(x=None, zh=None, zl=None, yy=None, c=None):
+        x = mission if x is None else x
+        zh = half if zh is None else zh
+        zl = near if zl is None else zl
+        yy = y if yy is None else yy
+        c = core if c is None else c
+        return (x, ((zh * 2 + zl) * 2 + yy) * 2 + c)
+
+    x_peer = device(x=1 - mission)
+    z_peer = device(zh=1 - half)
+    sibling = device(c=1 - core)
+    y_peer = device(yy=1 - y)
+    near_peer = device(zl=1 - near)
+    cross_peer = device(zl=1 - near, yy=1 - y)
+
+    def block(slot, at):
+        span = pl.ds(at * rows, rows)
+        return proj.at[span] if slot == TILES else gath.at[slot, span]
+
+    def remote(src, dst, send, recv, target):
+        return pltpu.make_async_remote_copy(
+            src_ref=src,
+            dst_ref=dst,
+            send_sem=send,
+            recv_sem=recv,
+            device_id=target,
+            device_id_type=pl.DeviceIdType.MESH,
+        )
+
+    def z_copy(slot):
+        source = slot if slot == TILES else SWAPPED[slot]
+        return remote(block(source, 0), block(slot, 2), z_send.at[slot], z_recv.at[slot], z_peer)
+
+    def x_copy(slot):
+        return remote(block(slot, 0), block(slot, 4), x_send.at[slot], x_recv.at[slot], x_peer)
+
+    def relay(slot):
+        return remote(block(slot, 2), block(slot, 6), r_send.at[slot], r_recv.at[slot], x_peer)
+
+    def share(chip, slot):
+        return remote(
+            block(slot, 2 * chip),
+            block(slot, 2 * chip + 1),
+            d_send.at[chip, slot],
+            d_recv.at[chip, slot],
+            sibling,
+        )
+
+    def own_copy(slot):
+        start = tile_at(slot, half) * tile_cols
+        return pltpu.make_async_copy(
+            design_ref.at[:, pl.ds(pl.multiple_of(start, LANES), tile_cols)],
+            block(slot, 0),
+            own_sem.at[slot],
+        )
+
+    for slot in range(TILES):
+        own_copy(slot).start()
+    barrier = pltpu.get_barrier_semaphore()
+    peers = (x_peer, z_peer, sibling, y_peer, near_peer, cross_peer)
+    for peer in peers:
+        pl.semaphore_signal(barrier, inc=1, device_id=peer, device_id_type=pl.DeviceIdType.MESH)
+    ends = near == half
+
+    def apart(work):
+        pl.when(arc >= 0)(work)
+
+    @apart
+    def _():
+        state_ref[...] = projector_start(sizes_ref, kinds_ref, nuis_ref, arc_ref, kind_ref)
+
+    pl.semaphore_wait(barrier, len(peers))
+    for slot in range(TILES):
+        own_copy(slot).wait()
+    def run(side):
+        y_first, straight_jobs = Y_FIRST[side], STRAIGHT[side]
+
+        def stage_one(n, k):
+            if y_first[n]:
+                zl, yy, to, target = (near if k else 1 - near), 1 - y, (near if k else 1 - near), y_peer
+            else:
+                zl, yy, to, target = 1 - near, (y if k else 1 - y), (y if k else 1 - y), near_peer
+            return remote(
+                part.at[n, zl, yy], first_in.at[n, to], one_send.at[n, k], one_recv.at[n, k], target
+            )
+
+        def straight(n):
+            picks = (
+                (near, 1 - y, first_in.at[n, 0], y_peer),
+                (1 - near, y, first_in.at[n, 1], near_peer),
+                (1 - near, 1 - y, second_in.at[n], cross_peer),
+            )
+            at = straight_jobs.index(n)
+            return [
+                remote(part.at[n, zl, yy], dst, s_send.at[at, k], s_recv.at[at, k], target)
+                for k, (zl, yy, dst, target) in enumerate(picks)
+            ]
+
+        def stage_two(n):
+            target = near_peer if y_first[n] else y_peer
+            return remote(
+                second_out.at[n], second_in.at[n], two_send.at[n], two_recv.at[n], target
+            )
+
+        def held(n, mine):
+            if y_first[n]:
+                at = near if mine else 1 - near
+                return part[n, at, y].astype(jnp.float32) + first_in[n, at].astype(jnp.float32)
+            at = y if mine else 1 - y
+            return part[n, near, at].astype(jnp.float32) + first_in[n, at].astype(jnp.float32)
+
+        def vector_copy(k):
+            target = (y_peer, near_peer, cross_peer)[k]
+            to = (2 * near + 1 - y, 2 * (1 - near) + y, 2 * (1 - near) + 1 - y)[k]
+            return remote(vec.at[to], vec_in.at[k], v_send.at[k], v_recv.at[k], target)
+
+        first, last = 0, TILES - 1
+        def when(condition, work):
+            if condition is True:
+                work()
+            elif condition is not False:
+                pl.when(condition)(work)
+
+        def here(slot):
+            return {first: side == 0, last: half == 0 if side == 0 else False}.get(slot, True)
+
+        def at_x_peer(slot):
+            return {first: side == 1, last: half == 0 if side == 1 else False}.get(slot, True)
+
+        def to_z_peer(slot):
+            return half == 1 if slot == last else True
+
+        def by_z(slot):
+            return half == 0 if slot == last else True
+
+        def start_z(slot):
+            when(to_z_peer(slot), lambda: z_copy(slot).start())
+
+        def start_x(slot):
+            when(at_x_peer(slot), lambda: x_copy(slot).start())
+
+        def start_share(slot):
+            when(here(slot), lambda: share(0, slot).start())
+
+        def z_if(condition, slot):
+            extra = to_z_peer(slot)
+            both = condition if extra is True else jnp.logical_and(condition, extra)
+            pl.when(both)(z_copy(slot).start)
+
+        def z_end(slot):
+            z_if(ends, slot)
+
+        def z_mid(slot):
+            z_if(jnp.logical_not(ends), slot)
+
+        @scoped
+        def from_z(slot):
+            def pass_along():
+                z_copy(slot).wait_recv()
+                when(at_x_peer(slot), lambda: relay(slot).start())
+                when(here(slot), lambda: share(1, slot).start())
+
+            when(by_z(slot), pass_along)
+
+        @scoped
+        def from_x(slot):
+            def pass_along():
+                x_copy(slot).wait_recv()
+                share(2, slot).start()
+
+            when(here(slot), pass_along)
+
+        @scoped
+        def from_relay(slot):
+            def pass_along():
+                relay(slot).wait_recv()
+                share(3, slot).start()
+
+            when(here(slot), pass_along)
+
+        @scoped
+        def settled(slot):
+            def wait():
+                for chip in range(4):
+                    share(chip, slot).wait_recv()
+
+            when(here(slot), wait)
+
+        def solved(slot):
+            return jnp.concatenate(
+                [
+                    jnp.dot(
+                        proj[pl.ds(at * rows, rows), :][:, :rows],
+                        gath[slot, pl.ds(at * rows, rows), :],
+                        preferred_element_type=jnp.float32,
+                    )
+                    for at in range(2 * 4)
+                ],
+                axis=0,
+            )
+
+        @scoped
+        def make_lhs(mirrored):
+            turned[...] = solved(side + (3 - 2 * side) * mirrored).T.astype(jnp.bfloat16)
+            for to in range(4):
+                start = 2 * rows * to + rows * core
+                if mirrored:
+                    start = tile_cols - rows - start
+                picked = turned[pl.ds(pl.multiple_of(start, 16), rows), :]
+                if mirrored:
+                    picked = jnp.dot(
+                        flip_matrix(rows), picked, preferred_element_type=jnp.float32
+                    ).astype(jnp.bfloat16)
+                lhs[mirrored, pl.ds(to * rows, rows), :] = picked
+
+        def product(mirrored, slot):
+            out = jnp.dot(lhs[mirrored], gath[slot], preferred_element_type=jnp.float32)
+            if not mirrored:
+                return out
+            flip = flip_matrix(LANES)
+            out = out.astype(jnp.bfloat16)
+            return jnp.concatenate(
+                [
+                    jnp.dot(out[:, start : start + LANES], flip, preferred_element_type=jnp.float32)
+                    for start in range(tile_cols - LANES, -1, -LANES)
+                ],
+                axis=1,
+            )
+
+        def put(n, value):
+            part[n] = value.astype(jnp.bfloat16).reshape(2, 2, rows, tile_cols)
+
+        def send_out(n):
+            for copy in straight(n) if n in straight_jobs else [stage_one(n, 0), stage_one(n, 1)]:
+                copy.start()
+
+        def diagonal(n):
+            local = lax.broadcasted_iota(jnp.int32, (4 * rows, tile_cols), 0)
+            local = lax.div(local, rows) * (2 * rows) + lax.rem(local, rows) + rows * core
+            cols = lax.broadcasted_iota(jnp.int32, (4 * rows, tile_cols), 1)
+            put(n, jnp.where(cols >= local, product(0, side), product(1, 3 - side)))
+            send_out(n)
+
+        def above(n, slot):
+            put(n, product(0, slot))
+            send_out(n)
+
+        def mirrored(n, slot):
+            put(n, product(1, slot))
+            send_out(n)
+
+        def on_low(work):
+            if side == 0:
+                work()
+
+        def on_high(work):
+            if side == 1:
+                work()
+
+        def on(x, zh):
+            return pl.when(half == zh) if side == x else lambda work: None
+
+        @scoped
+        def jobs_at(slot):
+            if slot == 1:
+
+                @on_low
+                def _():
+                    above(0, 1)
+
+            elif slot == 2:
+
+                @on_low
+                def _():
+                    above(1, 2)
+
+                @on_high
+                def _():
+                    above(0, 2)
+                    make_lhs(1)
+                    diagonal(1)
+
+            elif slot == 3:
+
+                @on_low
+                def _():
+                    above(2, 3)
+                    make_lhs(1)
+                    diagonal(3)
+
+                @on_high
+                def _():
+                    above(2, 3)
+                    mirrored(3, 3)
+
+            elif slot == 4:
+                above(4, 4)
+
+                @on_high
+                def _():
+                    mirrored(5, 4)
+
+                @on(0, 1)
+                def _():
+                    mirrored(7, 4)
+
+            elif slot == 5:
+
+                @on_low
+                def _():
+                    above(5, 5)
+
+                @on_high
+                def _():
+                    above(6, 5)
+
+                @on(1, 1)
+                def _():
+                    mirrored(7, 5)
+
+            elif slot == 6:
+
+                @on_low
+                def _():
+                    above(6, 6)
+
+                @on(1, 0)
+                def _():
+                    above(7, 6)
+
+            else:
+
+                @on(0, 0)
+                def _():
+                    above(7, 7)
+
+        def out_tile(n):
+            def upper(slot):
+                return tile_at(slot, half)
+
+            def lower(slot):
+                return TILES - 1 - tile_at(slot, half)
+
+            def by_mission(one, two):
+                return two if side else one
+
+            return (
+                lambda: by_mission(upper(1), upper(2)),
+                lambda: by_mission(upper(2), group),
+                lambda: upper(3),
+                lambda: by_mission(group, lower(3)),
+                lambda: upper(4),
+                lambda: by_mission(upper(5), lower(4)),
+                lambda: by_mission(upper(6), upper(5)),
+                lambda: by_mission(
+                    upper(7) + half * (lower(4) - upper(7)),
+                    upper(6) + half * (lower(5) - upper(6)),
+                ),
+            )[n]()
+
+        @scoped
+        def pass_on(n):
+            stage_one(n, 0).wait_recv()
+            second_out[n] = held(n, False).astype(jnp.bfloat16)
+            stage_two(n).start()
+
+        @scoped
+        def finish(n):
+            start = pl.multiple_of(out_tile(n) * tile_cols, LANES)
+            if n in straight_jobs:
+                for copy in straight(n):
+                    copy.wait_recv()
+                total = part[n, near, y].astype(jnp.float32)
+                for block in (first_in[n, 0], first_in[n, 1], second_in[n]):
+                    total = total + block.astype(jnp.float32)
+                fold_ref[:, pl.ds(start, tile_cols)] = total
+                return
+            stage_one(n, 1).wait_recv()
+            stage_two(n).wait_recv()
+            fold_ref[:, pl.ds(start, tile_cols)] = held(n, True) + second_in[n].astype(jnp.float32)
+
+        @scoped
+        def vectors():
+            def by_place(a, b, c, d):
+                return (1 - half) * (b if side else a) + half * (d if side else c)
+
+            low = by_place(
+                slot_of(0, 0), slot_of(4, 0), slot_of(2, 1), slot_of(6, 1)
+            )
+            high = by_place(
+                slot_of(1, 0), slot_of(5, 0), slot_of(3, 1), slot_of(7, 1)
+            )
+            last = by_place(
+                slot_of(4, 0), slot_of(6, 0), slot_of(5, 1), slot_of(7, 1)
+            )
+            lines = [
+                jnp.dot(right_lhs[...], gath[slot], preferred_element_type=jnp.float32)[:1]
+                for slot in (low, high)
+            ]
+            reduced = solved(last).astype(jnp.bfloat16).astype(jnp.float32)
+            lines.append(
+                jnp.sum(gath[last].astype(jnp.float32) * reduced, axis=0, keepdims=True)
+            )
+            right = jnp.concatenate(lines[:2], axis=1)
+            for to in range(4):
+                parts = []
+                for line, width in ((right, 2 * rows), (lines[2], rows)):
+                    even, odd = (
+                        line[:, at * width : (at + 1) * width] for at in (2 * to, 2 * to + 1)
+                    )
+                    parts.append(jnp.where(core == 0, even, odd))
+                parts.append(jnp.zeros((1, vec.shape[2] - 3 * rows), jnp.float32))
+                vec[to, :1, :] = jnp.concatenate(parts, axis=1)
+            for k in range(3):
+                vector_copy(k).start()
+
+        def sweep(start, stop):
+            @apart
+            def _():
+                state_ref[...] = eliminate(state_ref[...], start, stop)
+
+        @scoped
+        def project():
+            @apart
+            def _():
+                proj[pl.ds(0, rows), :] = projector_end(state_ref[...], weight_ref, obs_ref)
+
+            z_copy(TILES).start()
+            x_copy(TILES).start()
+            share(0, TILES).start()
+
+        def gather_sent():
+            for slot in range(TILES + 1):
+                when(to_z_peer(slot), lambda: z_copy(slot).wait_send())
+                when(at_x_peer(slot), lambda: x_copy(slot).wait_send())
+                when(at_x_peer(slot), lambda: relay(slot).wait_send())
+                for chip in range(4):
+                    when(here(slot), lambda: share(chip, slot).wait_send())
+
+        def sum_sent(n):
+            for copy in straight(n) if n in straight_jobs else [stage_one(n, 0), stage_one(n, 1), stage_two(n)]:
+                copy.wait_send()
+
+        def right_side_row():
+            turned_rows = proj[...].astype(jnp.float32).T.astype(jnp.bfloat16)
+            right_lhs[...] = turned_rows[rows : rows + 16]
+
+        def add_vectors():
+            total = vec[2 * near + y, :1, :]
+            for k in range(3):
+                vector_copy(k).wait_recv()
+                total = total + vec_in[k, :1, :]
+            right_ref[...] = total[:, : 2 * rows]
+            tail_ref[...] = total[:, 2 * rows : 3 * rows]
+
+
+        if side == 0:
+            start_share(0)
+            start_x(0)
+            start_z(0)
+            start_z(1)
+            start_x(1)
+            start_x(4)
+            start_x(2)
+            sweep(0 * rows // 80, 16 * rows // 80)
+            sweep(16 * rows // 80, 32 * rows // 80)
+            start_share(3)
+            start_share(1)
+            sweep(32 * rows // 80, 48 * rows // 80)
+            sweep(48 * rows // 80, 64 * rows // 80)
+            sweep(64 * rows // 80, 80 * rows // 80)
+            from_x(0)
+            project()
+            z_mid(2)
+            from_x(TILES)
+            z_end(2)
+            from_z(0)
+            z_mid(3)
+            start_x(3)
+            start_share(4)
+            from_x(1)
+            from_z(TILES)
+            from_relay(0)
+            z_mid(4)
+            from_x(4)
+            from_z(1)
+            from_relay(TILES)
+            z_mid(7)
+            z_mid(5)
+            start_share(2)
+            z_end(3)
+            from_z(2)
+            from_relay(1)
+            settled(TILES)
+            right_side_row()
+            from_x(2)
+            start_x(5)
+            from_relay(2)
+            settled(1)
+            z_end(4)
+            from_x(3)
+            start_share(7)
+            settled(0)
+            z_mid(6)
+            make_lhs(0)
+            z_end(7)
+            jobs_at(1)
+            from_z(3)
+            settled(2)
+            jobs_at(2)
+            from_z(4)
+            from_relay(3)
+            start_x(6)
+            start_x(7)
+            from_x(5)
+            start_share(6)
+            z_end(5)
+            z_end(6)
+            settled(3)
+            jobs_at(3)
+            from_relay(4)
+            settled(4)
+            jobs_at(4)
+            from_x(7)
+            from_z(5)
+            pass_on(2)
+            from_z(7)
+            from_x(6)
+            pass_on(4)
+            pass_on(0)
+            from_relay(5)
+            pass_on(1)
+            from_z(6)
+            start_share(5)
+            pass_on(3)
+            from_relay(7)
+            settled(5)
+            settled(7)
+            jobs_at(5)
+            from_relay(6)
+            settled(6)
+            jobs_at(6)
+            jobs_at(7)
+            pass_on(6)
+            pass_on(5)
+            finish(4)
+            finish(1)
+            vectors()
+            pass_on(7)
+            finish(2)
+            finish(5)
+            finish(6)
+            gather_sent()
+            sum_sent(4)
+            sum_sent(1)
+            sum_sent(2)
+            sum_sent(5)
+            sum_sent(6)
+            finish(3)
+            finish(0)
+            add_vectors()
+            finish(7)
+            sum_sent(3)
+            sum_sent(0)
+            sum_sent(7)
+            for k in range(3):
+                vector_copy(k).wait_send()
+        else:
+            start_share(0)
+            start_x(0)
+            start_z(0)
+            start_z(1)
+            start_x(1)
+            start_x(4)
+            start_x(2)
+            sweep(0 * rows // 80, 16 * rows // 80)
+            sweep(16 * rows // 80, 32 * rows // 80)
+            start_share(3)
+            start_share(1)
+            sweep(32 * rows // 80, 48 * rows // 80)
+            sweep(48 * rows // 80, 64 * rows // 80)
+            sweep(64 * rows // 80, 80 * rows // 80)
+            from_x(0)
+            project()
+            z_mid(2)
+            from_x(TILES)
+            z_end(2)
+            from_z(0)
+            z_mid(3)
+            start_x(3)
+            start_share(4)
+            from_x(1)
+            from_z(TILES)
+            from_relay(0)
+            z_mid(4)
+            from_x(4)
+            from_z(1)
+            from_relay(TILES)
+            z_mid(7)
+            z_mid(5)
+            start_share(2)
+            z_end(3)
+            from_z(2)
+            from_relay(1)
+            settled(TILES)
+            right_side_row()
+            from_x(2)
+            start_x(5)
+            from_relay(2)
+            settled(1)
+            z_end(4)
+            from_x(3)
+            start_share(7)
+            settled(0)
+            z_mid(6)
+            make_lhs(0)
+            z_end(7)
+            jobs_at(1)
+            from_z(3)
+            settled(2)
+            jobs_at(2)
+            from_z(4)
+            from_relay(3)
+            start_x(6)
+            start_x(7)
+            from_x(5)
+            start_share(6)
+            z_end(5)
+            z_end(6)
+            settled(3)
+            jobs_at(3)
+            from_relay(4)
+            settled(4)
+            jobs_at(4)
+            from_x(7)
+            from_z(5)
+            pass_on(2)
+            from_z(7)
+            from_x(6)
+            pass_on(4)
+            pass_on(0)
+            from_relay(5)
+            pass_on(1)
+            from_z(6)
+            start_share(5)
+            pass_on(3)
+            from_relay(7)
+            settled(5)
+            settled(7)
+            jobs_at(5)
+            from_relay(6)
+            settled(6)
+            jobs_at(6)
+            jobs_at(7)
+            pass_on(6)
+            pass_on(5)
+            finish(4)
+            finish(1)
+            vectors()
+            pass_on(7)
+            finish(2)
+            finish(5)
+            finish(6)
+            gather_sent()
+            sum_sent(4)
+            sum_sent(1)
+            sum_sent(2)
+            sum_sent(5)
+            sum_sent(6)
+            finish(3)
+            finish(0)
+            add_vectors()
+            finish(7)
+            sum_sent(3)
+            sum_sent(0)
+            sum_sent(7)
+            for k in range(3):
+                vector_copy(k).wait_send()
+
+    @pl.when(mission == 0)
+    def _():
+        run(0)
+
+    @pl.when(mission == 1)
+    def _():
+        run(1)
+
+def on_paired_chips(
+    design,
+    nuisance_design,
+    observed,
+    arc_of_row,
+    nuis_size,
+    weight_index,
+    kind_weight,
+    mission_weight,
+):
+    rows, width_all = design.shape
+    wide = rounded_up(rows + 1, LANES)
+    tile_cols = width_all // TILES
+    stacked = 2 * 4 * rows
+    vec_cols = rounded_up(3 * rows, LANES)
+    vmem = pl.BlockSpec(memory_space=pltpu.VMEM)
+    smem = pl.BlockSpec(memory_space=pltpu.SMEM)
+    dma = pltpu.SemaphoreType.DMA
+    slots = TILES + 1
+
+    fold, right, tail = pl.pallas_call(
+        normals_kernel,
+        out_shape=(
+            pltpu.VMEM((rows, width_all), jnp.float32),
+            pltpu.VMEM((1, 2 * rows), jnp.float32),
+            pltpu.VMEM((1, rows), jnp.float32),
+        ),
+        in_specs=[smem, smem, vmem, pl.BlockSpec(memory_space=pl.ANY), vmem, vmem, vmem, vmem],
+        out_specs=(vmem, vmem, vmem),
+        scratch_shapes=[
+            pltpu.VMEM((TILES, stacked, tile_cols), jnp.bfloat16),
+            pltpu.VMEM((stacked, wide), jnp.bfloat16),
+            pltpu.VMEM((rows, wide), jnp.float32),
+            pltpu.VMEM((tile_cols, stacked), jnp.bfloat16),
+            pltpu.VMEM((2, 4 * rows, stacked), jnp.bfloat16),
+            pltpu.VMEM((16, stacked), jnp.bfloat16),
+            pltpu.VMEM((TILES, 2, 2, rows, tile_cols), jnp.bfloat16),
+            pltpu.VMEM((TILES, 2, rows, tile_cols), jnp.bfloat16),
+            pltpu.VMEM((TILES, rows, tile_cols), jnp.bfloat16),
+            pltpu.VMEM((TILES, rows, tile_cols), jnp.bfloat16),
+            pltpu.VMEM((4, 8, vec_cols), jnp.float32),
+            pltpu.VMEM((3, 8, vec_cols), jnp.float32),
+            dma((TILES,)),
+            dma((slots,)),
+            dma((slots,)),
+            dma((slots,)),
+            dma((slots,)),
+            dma((slots,)),
+            dma((slots,)),
+            dma((4, slots)),
+            dma((4, slots)),
+            dma((TILES, 2)),
+            dma((TILES, 2)),
+            dma((TILES,)),
+            dma((TILES,)),
+            dma((1, 3)),
+            dma((1, 3)),
+            dma((3,)),
+            dma((3,)),
+        ],
+        compiler_params=pltpu.CompilerParams(
+            collective_id=0, has_side_effects=True, vmem_limit_bytes=60 * 2**20
+        ),
+        name="normals",
+    )(
+        nuis_size,
+        kind_weight,
+        mission_weight,
+        design,
+        nuisance_design,
+        arc_of_row,
+        weight_index,
+        observed,
+    )
+    return fold, right.reshape(-1), tail.reshape(-1)
+
+
 def solution(mesh):
     placed = (
         P(("mission", "arc"), None),
@@ -352,6 +1249,15 @@
         P(),
         P("mission"),
     )
+
+    def on_device(design, *rest):
+        devices = lax.axis_size("mission") * lax.axis_size("arc")
+        paired = lax.axis_size("mission") == 2 and lax.axis_size("arc") == 16
+        rows, width_all = design.shape
+        if paired and width_all == 2 * devices * rows and rows % 16 == 0 and width_all % (TILES * LANES) == 0:
+            return on_paired_chips(design, *rest)
+        return on_any_mesh(design, *rest)
+
     return jax.shard_map(
         on_device,
         mesh=mesh,

time: 156 us -> 68.5 us (0.44)
  waiting for transfers between devices: 48.3 us -> 0 us
  Pallas kernels: 37.1 us -> 64.7 us
  local copies, waits for them, and re-layouts: 22.2 us -> 2.24 us
  blocking collectives: 18.3 us -> 0 us
  between operations: 16.3 us -> 1.29 us
  starting transfers between devices: 7.15 us -> 0 us
  other arithmetic: 5.23 us -> 0 us
    all_gather x1 -> x0, waiting for transfers between devices: 29.8 us -> none  [gathered(): lax.all_gather(array, 'arc', axis=0, tiled=True, axis_index_groups=gather...]
    pallas_call x3 -> x1, Pallas kernels: 37.1 us -> 64.7 us  [on_paired_chips(): pl.pallas_call(normals_kernel, out_shape=(pltpu.VMEM((rows, width_all), j...]
    all_gather x1 -> x0, blocking collectives: 18.3 us -> none  [gathered(): lax.all_gather(array, 'arc', axis=0, tiled=True, axis_index_groups=gather...]
    ppermute x6 -> x0, waiting for transfers between devices: 17.9 us -> none  [the longest x3 17.9 us: on_device(): vector = lax.ppermute(vector, ('mission', 'arc'), ring(dm, dy))]
    ppermute x6 -> x0, starting transfers between devices: 7.12 us -> none  [the longest x3 3.62 us: on_device(): block = lax.ppermute(block, ('mission', 'arc'), ring(dm, dy))]
    concatenate x2 -> x0, local copies, waits for them, and re-layouts: 6.62 us -> none  [fold_call(): jnp.concatenate(picked(lambda block: block * final_rows) + picked(lambda...]
    broadcast_in_dim x4 -> x0, local copies, waits for them, and re-layouts: 5.07 us -> none  [the longest x1 1.36 us: on_device(): arc_of_row[:, None]]
    dynamic_slice x2 -> x0, local copies, waits for them, and re-layouts: 4.64 us -> none  [the longest x1 3.82 us: picked(): lax.dynamic_slice_in_dim(design_all, start_of(owner), final_rows, 1)]
  transfers between devices with their start and end apart: 7 -> 0, of which waited for: 3 -> 0; matrix products, arithmetic and copies ran while one was open for 11% -> 0% of each run, Pallas kernels for 16% -> 0%
where the time goes in v3:
time: 68.5 us; the launch traced here: 68.3 us
  Pallas kernels  64.7 us (94%)
  local copies, waits for them, and re-layouts  2.24 us (3%)
  between operations  1.29 us (2%)
    pallas_call x1, Pallas kernels, on_paired_chips(): pl.pallas_call(normals_kernel, out_shape=(pltpu.VMEM((rows, width_all), j...  64.7 us
    unnamed x3, local copies, waits for them, and re-layouts  2.24 us

profile of v3, /device:TPU:0, one launch (start us, length us, event | category | flops | bytes accessed | tf_op | source)
XLA Modules:
  0.0 68.3 jit_solution(10351547323201561529)
XLA Ops:
  1.3 64.7 %normals.1 = (f32[80,5120]{1,0:T(8,128)S(1)}, f32[1,160]{1,0:T(1,128)S(1)}, f32[1,80]{1,0:T(1,128)S(1)}) custom-call(s32[2]{0:T(128)} %sizes_ref.1, f32[8]{0:T(128)} %kinds_ref.1, f32[1]{0:T(128)S(6)} %copy.17.weight_ref, bf16[80,5120]{1,0:T(8,128)(2,1)} %design_ref.1, bf16[80,128]{1,0:T(8,128)(2,1)} %nuis_ref.1, s32[80]{0:T(128)} %arc_ref.1, s32[80]{0:T(128)} %kind_ref.1, ...), custom_call_target="tpu_custom_call" | custom-call | tf_op jit(solution)/shard_map/normals/pallas_call | solution.py:1184
  66.0 1.2 %copy.14 = f32[80,5120]{1,0:T(8,128)} copy(f32[80,5120]{1,0:T(8,128)S(1)} %get-tuple-element.9) | data formatting | bytes 3276800
  67.2 0.6 copy.15
  67.8 0.5 copy.16

commit v4 on v3

--- a/solution.py
+++ b/solution.py
@@ -344,8 +344,8 @@
 TILES = 8
 ARRIVAL = (0, 2, 5, 7, 6, 4, 3, 1)
 Y_FIRST = (
-    (True, False, True, False, True, True, False, True,),
-    (True, False, True, False, True, True, False, True,),
+    (True, False, True, True, True, False, True, False,),
+    (True, False, True, True, True, False, True, False,),
 )
 STRAIGHT = ((), ())
 SWAPPED = tuple(ARRIVAL.index(tile ^ 1) for tile in ARRIVAL)
@@ -931,225 +931,225 @@
 
 
         if side == 0:
-            start_share(0)
-            start_x(0)
-            start_z(0)
-            start_z(1)
-            start_x(1)
-            start_x(4)
-            start_x(2)
-            sweep(0 * rows // 80, 16 * rows // 80)
-            sweep(16 * rows // 80, 32 * rows // 80)
             start_share(3)
             start_share(1)
+            start_x(1)
+            start_z(1)
+            sweep(0 * rows // 80, 16 * rows // 80)
+            start_x(2)
+            sweep(16 * rows // 80, 32 * rows // 80)
+            start_share(4)
             sweep(32 * rows // 80, 48 * rows // 80)
+            start_z(0)
+            start_share(6)
             sweep(48 * rows // 80, 64 * rows // 80)
             sweep(64 * rows // 80, 80 * rows // 80)
+            from_z(1)
             from_x(0)
+            start_share(0)
+            start_share(5)
+            start_x(3)
+            z_mid(2)
+            z_end(2)
+            start_share(2)
+            start_x(4)
             project()
-            z_mid(2)
-            from_x(TILES)
-            z_end(2)
+            z_mid(3)
+            start_x(0)
+            from_z(TILES)
             from_z(0)
-            z_mid(3)
-            start_x(3)
-            start_share(4)
-            from_x(1)
-            from_z(TILES)
+            z_mid(4)
+            from_x(2)
             from_relay(0)
-            z_mid(4)
-            from_x(4)
-            from_z(1)
-            from_relay(TILES)
-            z_mid(7)
-            z_mid(5)
-            start_share(2)
             z_end(3)
             from_z(2)
+            from_x(1)
+            from_x(TILES)
+            z_mid(5)
+            z_end(4)
+            start_share(7)
+            from_relay(TILES)
+            settled(0)
             from_relay(1)
             settled(TILES)
-            right_side_row()
-            from_x(2)
-            start_x(5)
-            from_relay(2)
+            from_x(4)
             settled(1)
-            z_end(4)
-            from_x(3)
-            start_share(7)
-            settled(0)
-            z_mid(6)
             make_lhs(0)
-            z_end(7)
             jobs_at(1)
             from_z(3)
+            from_relay(2)
+            right_side_row()
+            start_x(6)
+            z_end(5)
+            start_x(7)
+            start_x(5)
+            z_mid(6)
             settled(2)
             jobs_at(2)
             from_z(4)
+            z_end(7)
             from_relay(3)
-            start_x(6)
-            start_x(7)
-            from_x(5)
-            start_share(6)
-            z_end(5)
+            z_mid(7)
+            from_x(3)
             z_end(6)
             settled(3)
+            from_z(5)
             jobs_at(3)
+            pass_on(0)
             from_relay(4)
+            from_x(6)
             settled(4)
             jobs_at(4)
-            from_x(7)
-            from_z(5)
             pass_on(2)
+            from_x(5)
+            from_relay(5)
+            settled(5)
+            from_z(6)
             from_z(7)
-            from_x(6)
-            pass_on(4)
-            pass_on(0)
-            from_relay(5)
-            pass_on(1)
-            from_z(6)
-            start_share(5)
-            pass_on(3)
-            from_relay(7)
-            settled(5)
-            settled(7)
             jobs_at(5)
             from_relay(6)
+            from_x(7)
+            pass_on(1)
+            pass_on(3)
+            finish(0)
+            from_relay(7)
             settled(6)
             jobs_at(6)
+            finish(2)
+            pass_on(4)
+            settled(7)
             jobs_at(7)
+            vectors()
+            pass_on(5)
             pass_on(6)
-            pass_on(5)
+            finish(1)
+            pass_on(7)
             finish(4)
-            finish(1)
-            vectors()
-            pass_on(7)
-            finish(2)
+            finish(3)
+            gather_sent()
+            sum_sent(0)
+            sum_sent(2)
+            sum_sent(1)
+            sum_sent(4)
+            sum_sent(3)
+            finish(6)
             finish(5)
-            finish(6)
-            gather_sent()
-            sum_sent(4)
-            sum_sent(1)
-            sum_sent(2)
-            sum_sent(5)
-            sum_sent(6)
-            finish(3)
-            finish(0)
             add_vectors()
             finish(7)
-            sum_sent(3)
-            sum_sent(0)
+            sum_sent(6)
+            sum_sent(5)
             sum_sent(7)
             for k in range(3):
                 vector_copy(k).wait_send()
         else:
+            start_z(0)
+            from_x(0)
             start_share(0)
+            start_share(3)
+            sweep(0 * rows // 80, 16 * rows // 80)
             start_x(0)
-            start_z(0)
+            sweep(16 * rows // 80, 32 * rows // 80)
             start_z(1)
+            sweep(32 * rows // 80, 48 * rows // 80)
+            start_x(2)
+            start_share(7)
+            start_share(2)
+            sweep(48 * rows // 80, 64 * rows // 80)
+            start_share(5)
             start_x(1)
-            start_x(4)
-            start_x(2)
-            sweep(0 * rows // 80, 16 * rows // 80)
-            sweep(16 * rows // 80, 32 * rows // 80)
-            start_share(3)
+            sweep(64 * rows // 80, 80 * rows // 80)
+            project()
             start_share(1)
-            sweep(32 * rows // 80, 48 * rows // 80)
-            sweep(48 * rows // 80, 64 * rows // 80)
-            sweep(64 * rows // 80, 80 * rows // 80)
-            from_x(0)
-            project()
+            from_z(0)
             z_mid(2)
-            from_x(TILES)
-            z_end(2)
-            from_z(0)
+            from_z(TILES)
             z_mid(3)
-            start_x(3)
-            start_share(4)
+            from_z(1)
+            from_relay(1)
             from_x(1)
-            from_z(TILES)
+            z_mid(6)
             from_relay(0)
             z_mid(4)
+            z_end(2)
+            start_share(6)
+            settled(0)
+            start_x(4)
+            z_end(3)
+            start_share(4)
+            from_x(2)
+            z_end(4)
+            start_x(3)
+            settled(1)
+            from_z(2)
+            from_x(TILES)
+            from_relay(TILES)
+            settled(TILES)
+            from_relay(2)
+            make_lhs(0)
+            settled(2)
+            from_z(3)
+            from_x(3)
+            z_end(5)
+            jobs_at(1)
+            jobs_at(2)
+            start_x(6)
+            start_x(5)
+            from_relay(3)
+            settled(3)
+            z_mid(5)
+            jobs_at(3)
             from_x(4)
-            from_z(1)
-            from_relay(TILES)
             z_mid(7)
-            z_mid(5)
-            start_share(2)
-            z_end(3)
-            from_z(2)
-            from_relay(1)
-            settled(TILES)
             right_side_row()
-            from_x(2)
-            start_x(5)
-            from_relay(2)
-            settled(1)
-            z_end(4)
-            from_x(3)
-            start_share(7)
-            settled(0)
-            z_mid(6)
-            make_lhs(0)
+            pass_on(0)
+            from_z(4)
+            z_end(6)
+            from_x(6)
+            from_relay(4)
+            from_z(5)
+            settled(4)
+            settled(7)
             z_end(7)
-            jobs_at(1)
-            from_z(3)
-            settled(2)
-            jobs_at(2)
-            from_z(4)
-            from_relay(3)
-            start_x(6)
+            jobs_at(4)
+            from_relay(5)
             start_x(7)
             from_x(5)
-            start_share(6)
-            z_end(5)
-            z_end(6)
-            settled(3)
-            jobs_at(3)
-            from_relay(4)
-            settled(4)
-            jobs_at(4)
-            from_x(7)
-            from_z(5)
             pass_on(2)
-            from_z(7)
-            from_x(6)
-            pass_on(4)
-            pass_on(0)
-            from_relay(5)
+            pass_on(3)
+            settled(5)
             pass_on(1)
             from_z(6)
-            start_share(5)
-            pass_on(3)
-            from_relay(7)
-            settled(5)
-            settled(7)
             jobs_at(5)
+            from_z(7)
             from_relay(6)
             settled(6)
+            pass_on(4)
+            pass_on(5)
             jobs_at(6)
+            vectors()
+            finish(3)
+            finish(0)
+            pass_on(6)
+            pass_on(7)
+            finish(4)
+            finish(7)
+            finish(1)
+            from_x(7)
+            gather_sent()
+            sum_sent(3)
+            sum_sent(0)
+            sum_sent(4)
+            sum_sent(7)
+            sum_sent(1)
+            finish(6)
             jobs_at(7)
-            pass_on(6)
-            pass_on(5)
-            finish(4)
-            finish(1)
-            vectors()
-            pass_on(7)
             finish(2)
+            from_relay(7)
+            add_vectors()
             finish(5)
-            finish(6)
-            gather_sent()
-            sum_sent(4)
-            sum_sent(1)
+            sum_sent(6)
             sum_sent(2)
             sum_sent(5)
-            sum_sent(6)
-            finish(3)
-            finish(0)
-            add_vectors()
-            finish(7)
-            sum_sent(3)
-            sum_sent(0)
-            sum_sent(7)
             for k in range(3):
                 vector_copy(k).wait_send()
 

time: 68.5 us -> 67.8 us (0.990)
  no operation moved by 1% of the time
where the time goes in v4:
time: 67.8 us; the launch traced here: 67.6 us
  Pallas kernels  64.1 us (95%)
  local copies, waits for them, and re-layouts  2.24 us (3%)
  between operations  1.29 us (2%)
    pallas_call x1, Pallas kernels, on_paired_chips(): pl.pallas_call(normals_kernel, out_shape=(pltpu.VMEM((rows, width_all), j...  64.1 us
    unnamed x3, local copies, waits for them, and re-layouts  2.24 us

profile of v4, /device:TPU:0, one launch (start us, length us, event | category | flops | bytes accessed | tf_op | source)
XLA Modules:
  0.0 67.6 jit_solution(16618306376416224472)
XLA Ops:
  1.3 64.1 %normals.1 = (f32[80,5120]{1,0:T(8,128)S(1)}, f32[1,160]{1,0:T(1,128)S(1)}, f32[1,80]{1,0:T(1,128)S(1)}) custom-call(s32[2]{0:T(128)} %sizes_ref.1, f32[8]{0:T(128)} %kinds_ref.1, f32[1]{0:T(128)S(6)} %copy.17.weight_ref, bf16[80,5120]{1,0:T(8,128)(2,1)} %design_ref.1, bf16[80,128]{1,0:T(8,128)(2,1)} %nuis_ref.1, s32[80]{0:T(128)} %arc_ref.1, s32[80]{0:T(128)} %kind_ref.1, ...), custom_call_target="tpu_custom_call" | custom-call | tf_op jit(solution)/shard_map/normals/pallas_call | solution.py:1184
  65.4 1.2 %copy.14 = f32[80,5120]{1,0:T(8,128)} copy(f32[80,5120]{1,0:T(8,128)S(1)} %get-tuple-element.9) | data formatting | bytes 3276800
  66.6 0.6 copy.15
  67.1 0.5 copy.16
